TPU v7x, 256 devices: a whole 4x4x8 slice. The times are simulated.
256 devices in a mesh: ka: 32 (over z, x_lo, core), sp: 8 (over y, x_hi).
Axes of the slice: x: 4 (x_hi: 2, x_lo: 2; x = x_hi * 2 + x_lo), y: 4, z: 8, core: 2. Of those that a mesh axis runs over, the one named last changes fastest.
Arguments:
- bloch_index: int32 [32, 2], P('ka'), may hold values from 0 to 63
- material: int32 [128, 64, 128], P('sp'), may hold values from 0 to 2
- permittivity: float32 [3], replicated, may hold values from 1 to 12
- absorption_peak: float32 [1], replicated, may hold values from 0.25 to 2
- source_sheet: float32 [32, 2, 128, 64], P('ka', None, 'sp'), may hold values from -6 to 6
- waveform: float32 [10], replicated, may hold values from -6 to 6
- electric_in: bfloat16 [32, 6, 128, 64, 128], P('ka', None, 'sp'), may hold values from -12 to 12
- magnetic_in: bfloat16 [32, 6, 128, 64, 128], P('ka', None, 'sp'), may hold values from -12 to 12
Outputs:
- electric_out: float32 [32, 6, 128, 64, 128], P('ka', None, 'sp')
- magnetic_out: float32 [32, 6, 128, 64, 128], P('ka', None, 'sp')
- reflected: float32 [32, 2], P('ka')
- reflected_mean: float32 [2], replicated
All inputs are finite; a program needn't handle non-finite values.
Results may differ from a plain program's by a relative error of at most 0.0003.
Values sent between devices are 32-bit elements; how exact they have to be, the bound alone decides.
A program may use at most 64 MiB of HBM per device.

v0:
```python
import jax
import jax.numpy as jnp
from jax import lax
from jax.sharding import PartitionSpec as P

PML = 16
INTERVAL = 5
NSNAP = 2
MPHASE = 64
NMAT = 3


TIME_STEP = 0.5


def shifted_2(value, axis, steps):
    count = lax.axis_size(axis)
    pairs = [(source, (source + steps) % count) for source in range(count)]
    return lax.ppermute(value, axis, pairs)


def sent_to_all(shard, axis):
    copies = jnp.broadcast_to(shard, (lax.axis_size(axis), *shard.shape))
    return lax.all_to_all(copies, axis, split_axis=0, concat_axis=0, tiled=True)


def of_everyone(shard, axis):
    return sent_to_all(shard, axis).sum(axis=0)


def rotate(couple, cosine, sine):
    return (couple[0] * cosine - couple[1] * sine, couple[0] * sine + couple[1] * cosine)


def subtract(left, right):
    return (left[0] - right[0], left[1] - right[1])


def position(values, along):
    return lax.broadcasted_iota(jnp.int32, values.shape, along)


def roll_couple(couple, amount, along):
    return tuple((jnp.roll(values, amount, axis=along) for values in couple))


def above_cell(couple, beyond, along):
    length = couple[0].shape[along]
    rolled = roll_couple(couple, -1, along)
    last = position(couple[0], along) == length - 1
    return tuple((jnp.where(last, edge, moved) for edge, moved in zip(beyond, rolled)))


def below_cell(couple, beyond, along):
    rolled = roll_couple(couple, 1, along)
    first = position(couple[0], along) == 0
    return tuple((jnp.where(first, edge, moved) for edge, moved in zip(beyond, rolled)))


def forward_wrap(couple, along, cosine, sine):
    length = couple[0].shape[along]
    rolled = roll_couple(couple, -1, along)
    turned = rotate(rolled, cosine, sine)
    last = position(couple[0], along) == length - 1
    shifted = tuple((jnp.where(last, edge, moved) for edge, moved in zip(turned, rolled)))
    return subtract(shifted, couple)


def backward_wrap(couple, along, cosine, sine):
    rolled = roll_couple(couple, 1, along)
    turned = rotate(rolled, cosine, -sine)
    first = position(couple[0], along) == 0
    shifted = tuple((jnp.where(first, edge, moved) for edge, moved in zip(turned, rolled)))
    return subtract(couple, shifted)


def forward_open(couple):
    along = couple[0].ndim - 1
    length = couple[0].shape[along]
    rolled = roll_couple(couple, -1, along)
    last = position(couple[0], along) == length - 1
    shifted = tuple((jnp.where(last, 0.0, moved) for moved in rolled))
    return subtract(shifted, couple)


def backward_open(couple):
    along = couple[0].ndim - 1
    rolled = roll_couple(couple, 1, along)
    first = position(couple[0], along) == 0
    shifted = tuple((jnp.where(first, 0.0, moved) for moved in rolled))
    return subtract(couple, shifted)


def electric_curl(electric, beyond_y, beyond_z, cosine, sine):
    ex_part, ey_part, ez_part = electric
    across = ex_part[0].ndim - 3
    sideways = across + 1
    dx_ey = subtract(above_cell(ey_part, beyond_y, across), ey_part)
    dx_ez = subtract(above_cell(ez_part, beyond_z, across), ez_part)
    return (
        subtract(forward_wrap(ez_part, sideways, cosine, sine), forward_open(ey_part)),
        subtract(forward_open(ex_part), dx_ez),
        subtract(dx_ey, forward_wrap(ex_part, sideways, cosine, sine)),
    )


def magnetic_curl(magnetic, behind_y, behind_z, cosine, sine):
    hx_part, hy_part, hz_part = magnetic
    across = hx_part[0].ndim - 3
    sideways = across + 1
    bx_hy = subtract(hy_part, below_cell(hy_part, behind_y, across))
    bx_hz = subtract(hz_part, below_cell(hz_part, behind_z, across))
    return (
        subtract(backward_wrap(hz_part, sideways, cosine, sine), backward_open(hy_part)),
        subtract(backward_open(hx_part), bx_hz),
        subtract(bx_hy, backward_wrap(hx_part, sideways, cosine, sine)),
    )


def relax(couple, change, retain, factor):
    return (retain * couple[0] + factor * change[0], retain * couple[1] + factor * change[1])


def coefficients(material, permittivity, absorption_peak, depth):
    height = jnp.arange(depth, dtype=jnp.float32)
    low_depth = jnp.maximum(PML - height, 0.0) / PML
    high_depth = jnp.maximum(height - (depth - 1 - PML), 0.0) / PML
    conduct = absorption_peak[0] * (low_depth**3 + high_depth**3)
    half_mag = conduct * (0.5 * TIME_STEP)
    h_retain = (1.0 - half_mag) / (1.0 + half_mag)
    h_factor = -TIME_STEP / (1.0 + half_mag)
    relative = jnp.zeros(material.shape, jnp.float32)
    for level in range(NMAT):
        relative = relative + jnp.where(material == level, permittivity[level], 0.0)
    half_ele = conduct * (0.5 * TIME_STEP) / relative
    e_retain = (1.0 - half_ele) / (1.0 + half_ele)
    e_factor = TIME_STEP / relative / (1.0 + half_ele)
    return (e_retain, e_factor, h_retain, h_factor)


def split_plane(stacked, member):
    return (stacked[:, 2 * member : 2 * member + 1], stacked[:, 2 * member + 1 : 2 * member + 2])


def on_device(
    bloch_index,
    material,
    permittivity,
    absorption_peak,
    source_sheet,
    waveform,
    electric_in,
    magnetic_in,
):
    points = bloch_index.shape[0]
    rows, width, depth = material.shape
    e_retain, e_factor, h_retain, h_factor = coefficients(
        material, permittivity, absorption_peak, depth
    )
    plane = (jnp.arange(depth) == PML + 2).astype(jnp.float32)
    monitor = PML + 6
    angles = 2.0 * jnp.pi * bloch_index.astype(jnp.float32) / MPHASE
    cos_x = jnp.cos(angles[:, 0]).reshape(points, 1, 1, 1)
    sin_x = jnp.sin(angles[:, 0]).reshape(points, 1, 1, 1)
    cos_y = jnp.cos(angles[:, 1]).reshape(points, 1, 1, 1)
    sin_y = jnp.sin(angles[:, 1]).reshape(points, 1, 1, 1)
    slab = lax.axis_index("sp")
    slabs = lax.axis_size("sp")
    at_end = slab == slabs - 1
    at_start = slab == 0
    end_cos = jnp.where(at_end, cos_x, 1.0)
    end_sin = jnp.where(at_end, sin_x, 0.0)
    start_cos = jnp.where(at_start, cos_x, 1.0)
    start_sin = jnp.where(at_start, -sin_x, 0.0)
    sheet = (source_sheet[:, 0][..., None] * plane, source_sheet[:, 1][..., None] * plane)
    total_points = points * lax.axis_size("ka")
    cells_plane = rows * slabs * width

    def advance(fields, drive):
        electric, magnetic = fields
        front_plane = jnp.stack(
            [
                electric[1][0][:, 0],
                electric[1][1][:, 0],
                electric[2][0][:, 0],
                electric[2][1][:, 0],
            ],
            1,
        )
        received = shifted_2(front_plane, "sp", -1)
        beyond_y = rotate(split_plane(received, 0), end_cos, end_sin)
        beyond_z = rotate(split_plane(received, 1), end_cos, end_sin)
        change = electric_curl(electric, beyond_y, beyond_z, cos_y, sin_y)
        magnetic = tuple(
            (
                relax(couple, change_part, h_retain, h_factor)
                for couple, change_part in zip(magnetic, change)
            )
        )
        back_plane = jnp.stack(
            [
                magnetic[1][0][:, rows - 1],
                magnetic[1][1][:, rows - 1],
                magnetic[2][0][:, rows - 1],
                magnetic[2][1][:, rows - 1],
            ],
            1,
        )
        behind = shifted_2(back_plane, "sp", 1)
        behind_y = rotate(split_plane(behind, 0), start_cos, start_sin)
        behind_z = rotate(split_plane(behind, 1), start_cos, start_sin)
        change = magnetic_curl(magnetic, behind_y, behind_z, cos_y, sin_y)
        first_change = (change[0][0] - drive * sheet[0], change[0][1] - drive * sheet[1])
        change = (first_change, change[1], change[2])
        electric = tuple(
            (
                relax(couple, change_part, e_retain, e_factor)
                for couple, change_part in zip(electric, change)
            )
        )
        return (electric, magnetic)

    def snapshot(fields, index):
        fields = lax.fori_loop(
            0,
            INTERVAL,
            lambda inner, held: advance(held, waveform[index * INTERVAL + inner]),
            fields,
        )
        electric = fields[0]
        power = (
            electric[0][0][..., monitor] ** 2
            + electric[0][1][..., monitor] ** 2
            + electric[1][0][..., monitor] ** 2
            + electric[1][1][..., monitor] ** 2
        )
        partial_value = jnp.sum(power, (1, 2)) / cells_plane
        return (fields, partial_value)

    electric_wide = electric_in.astype(jnp.float32)
    magnetic_wide = magnetic_in.astype(jnp.float32)
    start_e = tuple(
        ((electric_wide[:, 2 * member], electric_wide[:, 2 * member + 1]) for member in range(3))
    )
    start_h = tuple(
        ((magnetic_wide[:, 2 * member], magnetic_wide[:, 2 * member + 1]) for member in range(3))
    )
    final, reports = lax.scan(snapshot, (start_e, start_h), jnp.arange(NSNAP))
    reflected = of_everyone(jnp.transpose(reports), "sp")
    reflected_mean = of_everyone(jnp.sum(reflected, 0) / total_points, "ka")
    electric, magnetic = final
    electric_out = jnp.stack([values for couple in electric for values in couple], 1)
    magnetic_out = jnp.stack([values for couple in magnetic for values in couple], 1)
    return (electric_out, magnetic_out, reflected, reflected_mean)


def solution(mesh):
    in_specs = (
        P("ka", None),
        P("sp", None, None),
        P(),
        P(),
        P("ka", None, "sp", None),
        P(),
        P("ka", None, "sp", None, None),
        P("ka", None, "sp", None, None),
    )
    out_specs = (
        P("ka", None, "sp", None, None),
        P("ka", None, "sp", None, None),
        P("ka", None),
        P(),
    )
    return jax.shard_map(
        on_device, mesh=mesh, in_specs=in_specs, out_specs=out_specs, check_vma=False
    )
```

profile of v0, /device:TPU:1, one launch (start us, length us, event | category | flops | bytes accessed | tf_op | source)
XLA Modules:
  0.0 501.1 jit_solution(12222379286781655261)
XLA Ops:
  4.9 3.5 convert_element_type.18
  8.4 2.1 convert_element_type.19
  11.8 5.1 %slice_bitcast_fusion = (f32[1,16,64,128]{3,2,1,0:T(8,128)}, f32[1,16,64,128]{3,2,1,0:T(8,128)}, f32[1,16,64,128]{3,2,1,0:T(8,128)}, f32[1,16,64,128]{3,2,1,0:T(...) fusion(f32[1,6,16,64,128]{4,3,2,1,0:T(8,128)} %convert_element_, ...), kind=kLoop, calls=%fused_computation.127 | loop fusion | bytes 12582912 | tf_op jit(solution)/shard_map/squeeze | solution.py:246
  17.0 3.1 multiply_divide_fusion
  20.6 440.2 %while.90 = (s32[]{:T(128)}, f32[1,16,64,128]{3,2,1,0:T(8,128)S(1)}, f32[1,16,64,128]{3,2,1,0:T(8,128)S(1)}, f32[1,16,64,128]{3,2,1,0:T(8,128)S(1)}, f32[1,16,64...) while((s32[]{:T(128)}, ...), condition=%wide.region_4.5_spmd.clone.clone, body=%wide.region_0.4_spmd.clone.clone.sunk | while | flops 21113380 | bytes 123783040 | solution.py:248
  24.4 210.5 %while.91 = (s32[]{:T(128)}, f32[1,16,64,128]{3,2,1,0:T(8,128)S(1)}, f32[1,16,64,128]{3,2,1,0:T(8,128)S(1)}, f32[1,16,64,128]{3,2,1,0:T(8,128)S(1)}, f32[1,16,64...) while((s32[]{:T(128)}, ...), condition=%wide.region_2.2_spmd, body=%wide.region_1.1_spmd.sunk | while | flops 20840868 | bytes 118443480 | solution.py:224
  26.1 6.1 %collective-permute-start = (f32[1,4,64,128]{3,2,1,0:T(8,128)S(1)}, f32[1,4,64,128]{3,2,1,0:T(8,128)S(1)}, u32[]{:S(2)}, u32[]{:S(2)}) collective-permute-start(f32[1,4,64,128]{3,2,1,0:T(8,128)S(1)} %pad_maximum_fusion.12), channel_id=1, source_target_pairs={{0,7},{1,0},{2,1},{3,2},{4,3},{5,4},{6,5},{7,6},{8,15},{9,8},{10,9... | collective-permute-start | bytes 393224 | tf_op jit(solution)/shard_map/while/body/eval_jaxpr/while/body/eval_jaxpr/ppermute | solution.py:19
  49.6 1.4 dynamic_slice.19
  51.1 2.9 fusion.98
  58.5 1.4 fusion.96
  63.1 4.5 collective-permute-done.1
  90.7 1.4 dynamic_slice.19
  92.2 2.9 fusion.98
  99.6 1.4 fusion.96
  101.2 2.2 collective-permute-start.1
  106.3 2.5 collective-permute-done.1
  131.7 1.4 dynamic_slice.19
  133.2 2.9 fusion.98
  140.6 1.4 fusion.96
  142.3 2.2 collective-permute-start.1
  147.3 2.5 collective-permute-done.1
  172.8 1.4 dynamic_slice.19
  174.3 2.9 fusion.98
  181.7 1.4 fusion.96
  183.4 2.2 collective-permute-start.1
  188.4 2.5 collective-permute-done.1
  213.9 1.4 dynamic_slice.19
  215.4 2.9 fusion.98
  222.8 1.4 fusion.96
  224.5 2.2 collective-permute-start.1
  229.5 2.5 collective-permute-done.1
  237.8 1.4 copy.28
  240.6 1.4 fusion.95
  247.1 205.4 %while.91 = (s32[]{:T(128)}, f32[1,16,64,128]{3,2,1,0:T(8,128)S(1)}, f32[1,16,64,128]{3,2,1,0:T(8,128)S(1)}, f32[1,16,64,128]{3,2,1,0:T(8,128)S(1)}, f32[1,16,64...) while((s32[]{:T(128)}, ...), condition=%wide.region_2.2_spmd, body=%wide.region_1.1_spmd.sunk | while | flops 20840868 | bytes 118443480 | solution.py:224
  267.1 1.4 dynamic_slice.19
  268.6 2.9 fusion.98
  276.0 1.4 fusion.96
  277.7 2.2 collective-permute-start.1
  282.7 2.5 collective-permute-done.1
  308.2 1.4 dynamic_slice.19
  309.7 2.9 fusion.98
  317.1 1.4 fusion.96
  318.7 2.2 collective-permute-start.1
  323.8 2.5 collective-permute-done.1
  349.2 1.4 dynamic_slice.19
  350.7 2.9 fusion.98
  358.1 1.4 fusion.96
  359.8 2.2 collective-permute-start.1
  364.8 2.5 collective-permute-done.1
  390.3 1.4 dynamic_slice.19
  391.8 2.9 fusion.98
  399.2 1.4 fusion.96
  400.9 2.2 collective-permute-start.1
  405.9 2.5 collective-permute-done.1
  431.4 1.4 dynamic_slice.19
  432.9 2.9 fusion.98
  440.3 1.4 fusion.96
  442.0 2.2 collective-permute-start.1
  447.0 2.5 collective-permute-done.1
  455.3 1.4 copy.28
  458.1 1.4 fusion.95
  462.0 3.2 all-to-all-start
  472.4 20.3 %all-to-all-start.1 = ((f32[32,1,2]{2,1,0:T(1,128)}), f32[32,1,2]{2,1,0:T(1,128)S(1)}, u32[]{:S(2)}, u32[]{:S(2)}) async-start(f32[32,1,2]{2,1,0:T(1,128)} %broadcast_in_dim.204), calls=%async_computation.1 | async-start | bytes 32768 | tf_op jit(solution)/shard_map/all_to_all | solution.py:24
  493.5 7.0 %all-to-all-done.1 = f32[32,1,2]{2,1,0:T(1,128)S(1)} async-done(((f32[32,1,2]{2,1,0:T(1,128)}), f32[32,1,2]{2,1,0:T(1,128)S(1)}, u32[]{:S(2)}, u32[]{:S(2)}) %all-to-all-start.1) | async-done | bytes 288 | tf_op jit(solution)/shard_map/all_to_all | solution.py:24
  (1456 shorter events, 327.4 us)
Async XLA Ops:
  24.5 13.6 %copy-start.34 = (f32[128]{0:T(128)}, f32[128]{0:T(128)S(1)}, u32[]{:S(2)}) copy-start(f32[128]{0:T(128)S(1)} %get-tuple-element.1767) | copy-start | bytes 1540 | tf_op jit(solution)/shard_map/while/body/eval_jaxpr/while
  24.5 13.6 %copy-start.36 = (f32[128]{0:T(128)}, f32[128]{0:T(128)S(1)}, u32[]{:S(2)}) copy-start(f32[128]{0:T(128)S(1)} %get-tuple-element.1768) | copy-start | bytes 1540 | tf_op jit(solution)/shard_map/while/body/eval_jaxpr/while
  24.5 13.0 %copy-start.17 = (f32[1,16,64,128]{3,2,1,0:T(8,128)S(1)}, f32[1,16,64,128]{3,2,1,0:T(8,128)}, u32[]{:S(2)}) copy-start(f32[1,16,64,128]{3,2,1,0:T(8,128)} %get-tuple-element.1727) | copy-start | bytes 1572868 | tf_op jit(solution)/shard_map/while/body/eval_jaxpr/while
  26.1 24.9 %collective-permute-start = (f32[1,4,64,128]{3,2,1,0:T(8,128)S(1)}, f32[1,4,64,128]{3,2,1,0:T(8,128)S(1)}, u32[]{:S(2)}, u32[]{:S(2)}) collective-permute-start(f32[1,4,64,128]{3,2,1,0:T(8,128)S(1)} %pad_maximum_fusion.12), channel_id=1, source_target_pairs={{0,7},{1,0},{2,1},{3,2},{4,3},{5,4},{6,5},{7,6},{8,15},{9,8},{10,9... | collective-permute-start | bytes 393224 | tf_op jit(solution)/shard_map/while/body/eval_jaxpr/while/body/eval_jaxpr/ppermute | solution.py:19
  56.7 13.3 %copy-start.3 = (f32[1,16,64,128]{3,2,1,0:T(8,128)}, f32[1,16,64,128]{3,2,1,0:T(8,128)S(1)}, u32[]{:S(2)}) copy-start(f32[1,16,64,128]{3,2,1,0:T(8,128)S(1)} %fusion.97) | copy-start | bytes 1572868 | tf_op jit(solution)/shard_map/while/body/eval_jaxpr/while
  58.2 9.5 %copy-start.6 = (f32[1,16,64,128]{3,2,1,0:T(8,128)}, f32[1,16,64,128]{3,2,1,0:T(8,128)S(1)}, u32[]{:S(2)}) copy-start(f32[1,16,64,128]{3,2,1,0:T(8,128)S(1)} %fusion.100) | copy-start | bytes 1572868 | tf_op jit(solution)/shard_map/while/body/eval_jaxpr/while
  60.2 7.5 %collective-permute-start.1 = (f32[1,4,64,128]{3,2,1,0:T(8,128)S(1)}, f32[1,4,64,128]{3,2,1,0:T(8,128)S(1)}, u32[]{:S(2)}, u32[]{:S(2)}) collective-permute-start(f32[1,4,64,128]{3,2,1,0:T(8,128)S(1)} %pad_maximum_fusion.13), channel_id=1, source_target_pairs={{0,1},{1,2},{2,3},{3,4},{4,5},{5,6},{6,7},{7,0},{8,9},{9,10},{10,1... | collective-permute-start | bytes 393224 | tf_op jit(solution)/shard_map/while/body/eval_jaxpr/while/body/eval_jaxpr/ppermute | solution.py:19
  70.7 8.4 %copy-start.34 = (f32[128]{0:T(128)}, f32[128]{0:T(128)S(1)}, u32[]{:S(2)}) copy-start(f32[128]{0:T(128)S(1)} %get-tuple-element.1767) | copy-start | bytes 1540 | tf_op jit(solution)/shard_map/while/body/eval_jaxpr/while
  70.7 8.4 %copy-start.36 = (f32[128]{0:T(128)}, f32[128]{0:T(128)S(1)}, u32[]{:S(2)}) copy-start(f32[128]{0:T(128)S(1)} %get-tuple-element.1768) | copy-start | bytes 1540 | tf_op jit(solution)/shard_map/while/body/eval_jaxpr/while
  72.3 19.8 %collective-permute-start = (f32[1,4,64,128]{3,2,1,0:T(8,128)S(1)}, f32[1,4,64,128]{3,2,1,0:T(8,128)S(1)}, u32[]{:S(2)}, u32[]{:S(2)}) collective-permute-start(f32[1,4,64,128]{3,2,1,0:T(8,128)S(1)} %pad_maximum_fusion.12), channel_id=1, source_target_pairs={{0,7},{1,0},{2,1},{3,2},{4,3},{5,4},{6,5},{7,6},{8,15},{9,8},{10,9... | collective-permute-start | bytes 393224 | tf_op jit(solution)/shard_map/while/body/eval_jaxpr/while/body/eval_jaxpr/ppermute | solution.py:19
  97.8 13.3 %copy-start.3 = (f32[1,16,64,128]{3,2,1,0:T(8,128)}, f32[1,16,64,128]{3,2,1,0:T(8,128)S(1)}, u32[]{:S(2)}) copy-start(f32[1,16,64,128]{3,2,1,0:T(8,128)S(1)} %fusion.97) | copy-start | bytes 1572868 | tf_op jit(solution)/shard_map/while/body/eval_jaxpr/while
  99.3 9.5 %copy-start.6 = (f32[1,16,64,128]{3,2,1,0:T(8,128)}, f32[1,16,64,128]{3,2,1,0:T(8,128)S(1)}, u32[]{:S(2)}) copy-start(f32[1,16,64,128]{3,2,1,0:T(8,128)S(1)} %fusion.100) | copy-start | bytes 1572868 | tf_op jit(solution)/shard_map/while/body/eval_jaxpr/while
  101.2 7.5 %collective-permute-start.1 = (f32[1,4,64,128]{3,2,1,0:T(8,128)S(1)}, f32[1,4,64,128]{3,2,1,0:T(8,128)S(1)}, u32[]{:S(2)}, u32[]{:S(2)}) collective-permute-start(f32[1,4,64,128]{3,2,1,0:T(8,128)S(1)} %pad_maximum_fusion.13), channel_id=1, source_target_pairs={{0,1},{1,2},{2,3},{3,4},{4,5},{5,6},{6,7},{7,0},{8,9},{9,10},{10,1... | collective-permute-start | bytes 393224 | tf_op jit(solution)/shard_map/while/body/eval_jaxpr/while/body/eval_jaxpr/ppermute | solution.py:19
  111.7 8.4 %copy-start.34 = (f32[128]{0:T(128)}, f32[128]{0:T(128)S(1)}, u32[]{:S(2)}) copy-start(f32[128]{0:T(128)S(1)} %get-tuple-element.1767) | copy-start | bytes 1540 | tf_op jit(solution)/shard_map/while/body/eval_jaxpr/while
  111.8 8.4 %copy-start.36 = (f32[128]{0:T(128)}, f32[128]{0:T(128)S(1)}, u32[]{:S(2)}) copy-start(f32[128]{0:T(128)S(1)} %get-tuple-element.1768) | copy-start | bytes 1540 | tf_op jit(solution)/shard_map/while/body/eval_jaxpr/while
  113.4 19.8 %collective-permute-start = (f32[1,4,64,128]{3,2,1,0:T(8,128)S(1)}, f32[1,4,64,128]{3,2,1,0:T(8,128)S(1)}, u32[]{:S(2)}, u32[]{:S(2)}) collective-permute-start(f32[1,4,64,128]{3,2,1,0:T(8,128)S(1)} %pad_maximum_fusion.12), channel_id=1, source_target_pairs={{0,7},{1,0},{2,1},{3,2},{4,3},{5,4},{6,5},{7,6},{8,15},{9,8},{10,9... | collective-permute-start | bytes 393224 | tf_op jit(solution)/shard_map/while/body/eval_jaxpr/while/body/eval_jaxpr/ppermute | solution.py:19
  138.9 13.3 %copy-start.3 = (f32[1,16,64,128]{3,2,1,0:T(8,128)}, f32[1,16,64,128]{3,2,1,0:T(8,128)S(1)}, u32[]{:S(2)}) copy-start(f32[1,16,64,128]{3,2,1,0:T(8,128)S(1)} %fusion.97) | copy-start | bytes 1572868 | tf_op jit(solution)/shard_map/while/body/eval_jaxpr/while
  140.3 9.5 %copy-start.6 = (f32[1,16,64,128]{3,2,1,0:T(8,128)}, f32[1,16,64,128]{3,2,1,0:T(8,128)S(1)}, u32[]{:S(2)}) copy-start(f32[1,16,64,128]{3,2,1,0:T(8,128)S(1)} %fusion.100) | copy-start | bytes 1572868 | tf_op jit(solution)/shard_map/while/body/eval_jaxpr/while
  142.3 7.5 %collective-permute-start.1 = (f32[1,4,64,128]{3,2,1,0:T(8,128)S(1)}, f32[1,4,64,128]{3,2,1,0:T(8,128)S(1)}, u32[]{:S(2)}, u32[]{:S(2)}) collective-permute-start(f32[1,4,64,128]{3,2,1,0:T(8,128)S(1)} %pad_maximum_fusion.13), channel_id=1, source_target_pairs={{0,1},{1,2},{2,3},{3,4},{4,5},{5,6},{6,7},{7,0},{8,9},{9,10},{10,1... | collective-permute-start | bytes 393224 | tf_op jit(solution)/shard_map/while/body/eval_jaxpr/while/body/eval_jaxpr/ppermute | solution.py:19
  152.8 8.4 %copy-start.34 = (f32[128]{0:T(128)}, f32[128]{0:T(128)S(1)}, u32[]{:S(2)}) copy-start(f32[128]{0:T(128)S(1)} %get-tuple-element.1767) | copy-start | bytes 1540 | tf_op jit(solution)/shard_map/while/body/eval_jaxpr/while
  152.8 8.4 %copy-start.36 = (f32[128]{0:T(128)}, f32[128]{0:T(128)S(1)}, u32[]{:S(2)}) copy-start(f32[128]{0:T(128)S(1)} %get-tuple-element.1768) | copy-start | bytes 1540 | tf_op jit(solution)/shard_map/while/body/eval_jaxpr/while
  154.5 19.8 %collective-permute-start = (f32[1,4,64,128]{3,2,1,0:T(8,128)S(1)}, f32[1,4,64,128]{3,2,1,0:T(8,128)S(1)}, u32[]{:S(2)}, u32[]{:S(2)}) collective-permute-start(f32[1,4,64,128]{3,2,1,0:T(8,128)S(1)} %pad_maximum_fusion.12), channel_id=1, source_target_pairs={{0,7},{1,0},{2,1},{3,2},{4,3},{5,4},{6,5},{7,6},{8,15},{9,8},{10,9... | collective-permute-start | bytes 393224 | tf_op jit(solution)/shard_map/while/body/eval_jaxpr/while/body/eval_jaxpr/ppermute | solution.py:19
  179.9 13.3 %copy-start.3 = (f32[1,16,64,128]{3,2,1,0:T(8,128)}, f32[1,16,64,128]{3,2,1,0:T(8,128)S(1)}, u32[]{:S(2)}) copy-start(f32[1,16,64,128]{3,2,1,0:T(8,128)S(1)} %fusion.97) | copy-start | bytes 1572868 | tf_op jit(solution)/shard_map/while/body/eval_jaxpr/while
  181.4 9.5 %copy-start.6 = (f32[1,16,64,128]{3,2,1,0:T(8,128)}, f32[1,16,64,128]{3,2,1,0:T(8,128)S(1)}, u32[]{:S(2)}) copy-start(f32[1,16,64,128]{3,2,1,0:T(8,128)S(1)} %fusion.100) | copy-start | bytes 1572868 | tf_op jit(solution)/shard_map/while/body/eval_jaxpr/while
  183.4 7.5 %collective-permute-start.1 = (f32[1,4,64,128]{3,2,1,0:T(8,128)S(1)}, f32[1,4,64,128]{3,2,1,0:T(8,128)S(1)}, u32[]{:S(2)}, u32[]{:S(2)}) collective-permute-start(f32[1,4,64,128]{3,2,1,0:T(8,128)S(1)} %pad_maximum_fusion.13), channel_id=1, source_target_pairs={{0,1},{1,2},{2,3},{3,4},{4,5},{5,6},{6,7},{7,0},{8,9},{9,10},{10,1... | collective-permute-start | bytes 393224 | tf_op jit(solution)/shard_map/while/body/eval_jaxpr/while/body/eval_jaxpr/ppermute | solution.py:19
  193.9 8.4 %copy-start.34 = (f32[128]{0:T(128)}, f32[128]{0:T(128)S(1)}, u32[]{:S(2)}) copy-start(f32[128]{0:T(128)S(1)} %get-tuple-element.1767) | copy-start | bytes 1540 | tf_op jit(solution)/shard_map/while/body/eval_jaxpr/while
  193.9 8.4 %copy-start.36 = (f32[128]{0:T(128)}, f32[128]{0:T(128)S(1)}, u32[]{:S(2)}) copy-start(f32[128]{0:T(128)S(1)} %get-tuple-element.1768) | copy-start | bytes 1540 | tf_op jit(solution)/shard_map/while/body/eval_jaxpr/while
  195.5 19.8 %collective-permute-start = (f32[1,4,64,128]{3,2,1,0:T(8,128)S(1)}, f32[1,4,64,128]{3,2,1,0:T(8,128)S(1)}, u32[]{:S(2)}, u32[]{:S(2)}) collective-permute-start(f32[1,4,64,128]{3,2,1,0:T(8,128)S(1)} %pad_maximum_fusion.12), channel_id=1, source_target_pairs={{0,7},{1,0},{2,1},{3,2},{4,3},{5,4},{6,5},{7,6},{8,15},{9,8},{10,9... | collective-permute-start | bytes 393224 | tf_op jit(solution)/shard_map/while/body/eval_jaxpr/while/body/eval_jaxpr/ppermute | solution.py:19
  221.0 13.3 %copy-start.3 = (f32[1,16,64,128]{3,2,1,0:T(8,128)}, f32[1,16,64,128]{3,2,1,0:T(8,128)S(1)}, u32[]{:S(2)}) copy-start(f32[1,16,64,128]{3,2,1,0:T(8,128)S(1)} %fusion.97) | copy-start | bytes 1572868 | tf_op jit(solution)/shard_map/while/body/eval_jaxpr/while
  222.5 9.5 %copy-start.6 = (f32[1,16,64,128]{3,2,1,0:T(8,128)}, f32[1,16,64,128]{3,2,1,0:T(8,128)S(1)}, u32[]{:S(2)}) copy-start(f32[1,16,64,128]{3,2,1,0:T(8,128)S(1)} %fusion.100) | copy-start | bytes 1572868 | tf_op jit(solution)/shard_map/while/body/eval_jaxpr/while
  224.5 7.5 %collective-permute-start.1 = (f32[1,4,64,128]{3,2,1,0:T(8,128)S(1)}, f32[1,4,64,128]{3,2,1,0:T(8,128)S(1)}, u32[]{:S(2)}, u32[]{:S(2)}) collective-permute-start(f32[1,4,64,128]{3,2,1,0:T(8,128)S(1)} %pad_maximum_fusion.13), channel_id=1, source_target_pairs={{0,1},{1,2},{2,3},{3,4},{4,5},{5,6},{6,7},{7,0},{8,9},{9,10},{10,1... | collective-permute-start | bytes 393224 | tf_op jit(solution)/shard_map/while/body/eval_jaxpr/while/body/eval_jaxpr/ppermute | solution.py:19
  247.1 8.4 %copy-start.34 = (f32[128]{0:T(128)}, f32[128]{0:T(128)S(1)}, u32[]{:S(2)}) copy-start(f32[128]{0:T(128)S(1)} %get-tuple-element.1767) | copy-start | bytes 1540 | tf_op jit(solution)/shard_map/while/body/eval_jaxpr/while
  247.1 8.4 %copy-start.36 = (f32[128]{0:T(128)}, f32[128]{0:T(128)S(1)}, u32[]{:S(2)}) copy-start(f32[128]{0:T(128)S(1)} %get-tuple-element.1768) | copy-start | bytes 1540 | tf_op jit(solution)/shard_map/while/body/eval_jaxpr/while
  248.7 19.8 %collective-permute-start = (f32[1,4,64,128]{3,2,1,0:T(8,128)S(1)}, f32[1,4,64,128]{3,2,1,0:T(8,128)S(1)}, u32[]{:S(2)}, u32[]{:S(2)}) collective-permute-start(f32[1,4,64,128]{3,2,1,0:T(8,128)S(1)} %pad_maximum_fusion.12), channel_id=1, source_target_pairs={{0,7},{1,0},{2,1},{3,2},{4,3},{5,4},{6,5},{7,6},{8,15},{9,8},{10,9... | collective-permute-start | bytes 393224 | tf_op jit(solution)/shard_map/while/body/eval_jaxpr/while/body/eval_jaxpr/ppermute | solution.py:19
  274.2 13.3 %copy-start.3 = (f32[1,16,64,128]{3,2,1,0:T(8,128)}, f32[1,16,64,128]{3,2,1,0:T(8,128)S(1)}, u32[]{:S(2)}) copy-start(f32[1,16,64,128]{3,2,1,0:T(8,128)S(1)} %fusion.97) | copy-start | bytes 1572868 | tf_op jit(solution)/shard_map/while/body/eval_jaxpr/while
  275.7 9.5 %copy-start.6 = (f32[1,16,64,128]{3,2,1,0:T(8,128)}, f32[1,16,64,128]{3,2,1,0:T(8,128)S(1)}, u32[]{:S(2)}) copy-start(f32[1,16,64,128]{3,2,1,0:T(8,128)S(1)} %fusion.100) | copy-start | bytes 1572868 | tf_op jit(solution)/shard_map/while/body/eval_jaxpr/while
  277.7 7.5 %collective-permute-start.1 = (f32[1,4,64,128]{3,2,1,0:T(8,128)S(1)}, f32[1,4,64,128]{3,2,1,0:T(8,128)S(1)}, u32[]{:S(2)}, u32[]{:S(2)}) collective-permute-start(f32[1,4,64,128]{3,2,1,0:T(8,128)S(1)} %pad_maximum_fusion.13), channel_id=1, source_target_pairs={{0,1},{1,2},{2,3},{3,4},{4,5},{5,6},{6,7},{7,0},{8,9},{9,10},{10,1... | collective-permute-start | bytes 393224 | tf_op jit(solution)/shard_map/while/body/eval_jaxpr/while/body/eval_jaxpr/ppermute | solution.py:19
  288.2 8.4 %copy-start.34 = (f32[128]{0:T(128)}, f32[128]{0:T(128)S(1)}, u32[]{:S(2)}) copy-start(f32[128]{0:T(128)S(1)} %get-tuple-element.1767) | copy-start | bytes 1540 | tf_op jit(solution)/shard_map/while/body/eval_jaxpr/while
  288.2 8.4 %copy-start.36 = (f32[128]{0:T(128)}, f32[128]{0:T(128)S(1)}, u32[]{:S(2)}) copy-start(f32[128]{0:T(128)S(1)} %get-tuple-element.1768) | copy-start | bytes 1540 | tf_op jit(solution)/shard_map/while/body/eval_jaxpr/while
  289.8 19.8 %collective-permute-start = (f32[1,4,64,128]{3,2,1,0:T(8,128)S(1)}, f32[1,4,64,128]{3,2,1,0:T(8,128)S(1)}, u32[]{:S(2)}, u32[]{:S(2)}) collective-permute-start(f32[1,4,64,128]{3,2,1,0:T(8,128)S(1)} %pad_maximum_fusion.12), channel_id=1, source_target_pairs={{0,7},{1,0},{2,1},{3,2},{4,3},{5,4},{6,5},{7,6},{8,15},{9,8},{10,9... | collective-permute-start | bytes 393224 | tf_op jit(solution)/shard_map/while/body/eval_jaxpr/while/body/eval_jaxpr/ppermute | solution.py:19
  315.3 13.3 %copy-start.3 = (f32[1,16,64,128]{3,2,1,0:T(8,128)}, f32[1,16,64,128]{3,2,1,0:T(8,128)S(1)}, u32[]{:S(2)}) copy-start(f32[1,16,64,128]{3,2,1,0:T(8,128)S(1)} %fusion.97) | copy-start | bytes 1572868 | tf_op jit(solution)/shard_map/while/body/eval_jaxpr/while
  316.7 9.5 %copy-start.6 = (f32[1,16,64,128]{3,2,1,0:T(8,128)}, f32[1,16,64,128]{3,2,1,0:T(8,128)S(1)}, u32[]{:S(2)}) copy-start(f32[1,16,64,128]{3,2,1,0:T(8,128)S(1)} %fusion.100) | copy-start | bytes 1572868 | tf_op jit(solution)/shard_map/while/body/eval_jaxpr/while
  318.7 7.5 %collective-permute-start.1 = (f32[1,4,64,128]{3,2,1,0:T(8,128)S(1)}, f32[1,4,64,128]{3,2,1,0:T(8,128)S(1)}, u32[]{:S(2)}, u32[]{:S(2)}) collective-permute-start(f32[1,4,64,128]{3,2,1,0:T(8,128)S(1)} %pad_maximum_fusion.13), channel_id=1, source_target_pairs={{0,1},{1,2},{2,3},{3,4},{4,5},{5,6},{6,7},{7,0},{8,9},{9,10},{10,1... | collective-permute-start | bytes 393224 | tf_op jit(solution)/shard_map/while/body/eval_jaxpr/while/body/eval_jaxpr/ppermute | solution.py:19
  329.2 8.4 %copy-start.34 = (f32[128]{0:T(128)}, f32[128]{0:T(128)S(1)}, u32[]{:S(2)}) copy-start(f32[128]{0:T(128)S(1)} %get-tuple-element.1767) | copy-start | bytes 1540 | tf_op jit(solution)/shard_map/while/body/eval_jaxpr/while
  329.3 8.4 %copy-start.36 = (f32[128]{0:T(128)}, f32[128]{0:T(128)S(1)}, u32[]{:S(2)}) copy-start(f32[128]{0:T(128)S(1)} %get-tuple-element.1768) | copy-start | bytes 1540 | tf_op jit(solution)/shard_map/while/body/eval_jaxpr/while
  330.9 19.8 %collective-permute-start = (f32[1,4,64,128]{3,2,1,0:T(8,128)S(1)}, f32[1,4,64,128]{3,2,1,0:T(8,128)S(1)}, u32[]{:S(2)}, u32[]{:S(2)}) collective-permute-start(f32[1,4,64,128]{3,2,1,0:T(8,128)S(1)} %pad_maximum_fusion.12), channel_id=1, source_target_pairs={{0,7},{1,0},{2,1},{3,2},{4,3},{5,4},{6,5},{7,6},{8,15},{9,8},{10,9... | collective-permute-start | bytes 393224 | tf_op jit(solution)/shard_map/while/body/eval_jaxpr/while/body/eval_jaxpr/ppermute | solution.py:19
  356.4 13.3 %copy-start.3 = (f32[1,16,64,128]{3,2,1,0:T(8,128)}, f32[1,16,64,128]{3,2,1,0:T(8,128)S(1)}, u32[]{:S(2)}) copy-start(f32[1,16,64,128]{3,2,1,0:T(8,128)S(1)} %fusion.97) | copy-start | bytes 1572868 | tf_op jit(solution)/shard_map/while/body/eval_jaxpr/while
  357.8 9.5 %copy-start.6 = (f32[1,16,64,128]{3,2,1,0:T(8,128)}, f32[1,16,64,128]{3,2,1,0:T(8,128)S(1)}, u32[]{:S(2)}) copy-start(f32[1,16,64,128]{3,2,1,0:T(8,128)S(1)} %fusion.100) | copy-start | bytes 1572868 | tf_op jit(solution)/shard_map/while/body/eval_jaxpr/while
  359.8 7.5 %collective-permute-start.1 = (f32[1,4,64,128]{3,2,1,0:T(8,128)S(1)}, f32[1,4,64,128]{3,2,1,0:T(8,128)S(1)}, u32[]{:S(2)}, u32[]{:S(2)}) collective-permute-start(f32[1,4,64,128]{3,2,1,0:T(8,128)S(1)} %pad_maximum_fusion.13), channel_id=1, source_target_pairs={{0,1},{1,2},{2,3},{3,4},{4,5},{5,6},{6,7},{7,0},{8,9},{9,10},{10,1... | collective-permute-start | bytes 393224 | tf_op jit(solution)/shard_map/while/body/eval_jaxpr/while/body/eval_jaxpr/ppermute | solution.py:19
  370.3 8.4 %copy-start.34 = (f32[128]{0:T(128)}, f32[128]{0:T(128)S(1)}, u32[]{:S(2)}) copy-start(f32[128]{0:T(128)S(1)} %get-tuple-element.1767) | copy-start | bytes 1540 | tf_op jit(solution)/shard_map/while/body/eval_jaxpr/while
  370.3 8.4 %copy-start.36 = (f32[128]{0:T(128)}, f32[128]{0:T(128)S(1)}, u32[]{:S(2)}) copy-start(f32[128]{0:T(128)S(1)} %get-tuple-element.1768) | copy-start | bytes 1540 | tf_op jit(solution)/shard_map/while/body/eval_jaxpr/while
  372.0 19.8 %collective-permute-start = (f32[1,4,64,128]{3,2,1,0:T(8,128)S(1)}, f32[1,4,64,128]{3,2,1,0:T(8,128)S(1)}, u32[]{:S(2)}, u32[]{:S(2)}) collective-permute-start(f32[1,4,64,128]{3,2,1,0:T(8,128)S(1)} %pad_maximum_fusion.12), channel_id=1, source_target_pairs={{0,7},{1,0},{2,1},{3,2},{4,3},{5,4},{6,5},{7,6},{8,15},{9,8},{10,9... | collective-permute-start | bytes 393224 | tf_op jit(solution)/shard_map/while/body/eval_jaxpr/while/body/eval_jaxpr/ppermute | solution.py:19
  397.4 13.3 %copy-start.3 = (f32[1,16,64,128]{3,2,1,0:T(8,128)}, f32[1,16,64,128]{3,2,1,0:T(8,128)S(1)}, u32[]{:S(2)}) copy-start(f32[1,16,64,128]{3,2,1,0:T(8,128)S(1)} %fusion.97) | copy-start | bytes 1572868 | tf_op jit(solution)/shard_map/while/body/eval_jaxpr/while
  398.9 9.5 %copy-start.6 = (f32[1,16,64,128]{3,2,1,0:T(8,128)}, f32[1,16,64,128]{3,2,1,0:T(8,128)S(1)}, u32[]{:S(2)}) copy-start(f32[1,16,64,128]{3,2,1,0:T(8,128)S(1)} %fusion.100) | copy-start | bytes 1572868 | tf_op jit(solution)/shard_map/while/body/eval_jaxpr/while
  400.9 7.5 %collective-permute-start.1 = (f32[1,4,64,128]{3,2,1,0:T(8,128)S(1)}, f32[1,4,64,128]{3,2,1,0:T(8,128)S(1)}, u32[]{:S(2)}, u32[]{:S(2)}) collective-permute-start(f32[1,4,64,128]{3,2,1,0:T(8,128)S(1)} %pad_maximum_fusion.13), channel_id=1, source_target_pairs={{0,1},{1,2},{2,3},{3,4},{4,5},{5,6},{6,7},{7,0},{8,9},{9,10},{10,1... | collective-permute-start | bytes 393224 | tf_op jit(solution)/shard_map/while/body/eval_jaxpr/while/body/eval_jaxpr/ppermute | solution.py:19
  411.4 8.4 %copy-start.34 = (f32[128]{0:T(128)}, f32[128]{0:T(128)S(1)}, u32[]{:S(2)}) copy-start(f32[128]{0:T(128)S(1)} %get-tuple-element.1767) | copy-start | bytes 1540 | tf_op jit(solution)/shard_map/while/body/eval_jaxpr/while
  413.0 19.8 %collective-permute-start = (f32[1,4,64,128]{3,2,1,0:T(8,128)S(1)}, f32[1,4,64,128]{3,2,1,0:T(8,128)S(1)}, u32[]{:S(2)}, u32[]{:S(2)}) collective-permute-start(f32[1,4,64,128]{3,2,1,0:T(8,128)S(1)} %pad_maximum_fusion.12), channel_id=1, source_target_pairs={{0,7},{1,0},{2,1},{3,2},{4,3},{5,4},{6,5},{7,6},{8,15},{9,8},{10,9... | collective-permute-start | bytes 393224 | tf_op jit(solution)/shard_map/while/body/eval_jaxpr/while/body/eval_jaxpr/ppermute | solution.py:19
  438.5 13.3 %copy-start.3 = (f32[1,16,64,128]{3,2,1,0:T(8,128)}, f32[1,16,64,128]{3,2,1,0:T(8,128)S(1)}, u32[]{:S(2)}) copy-start(f32[1,16,64,128]{3,2,1,0:T(8,128)S(1)} %fusion.97) | copy-start | bytes 1572868 | tf_op jit(solution)/shard_map/while/body/eval_jaxpr/while
  440.0 9.5 %copy-start.6 = (f32[1,16,64,128]{3,2,1,0:T(8,128)}, f32[1,16,64,128]{3,2,1,0:T(8,128)S(1)}, u32[]{:S(2)}) copy-start(f32[1,16,64,128]{3,2,1,0:T(8,128)S(1)} %fusion.100) | copy-start | bytes 1572868 | tf_op jit(solution)/shard_map/while/body/eval_jaxpr/while
  442.0 7.5 %collective-permute-start.1 = (f32[1,4,64,128]{3,2,1,0:T(8,128)S(1)}, f32[1,4,64,128]{3,2,1,0:T(8,128)S(1)}, u32[]{:S(2)}, u32[]{:S(2)}) collective-permute-start(f32[1,4,64,128]{3,2,1,0:T(8,128)S(1)} %pad_maximum_fusion.13), channel_id=1, source_target_pairs={{0,1},{1,2},{2,3},{3,4},{4,5},{5,6},{6,7},{7,0},{8,9},{9,10},{10,1... | collective-permute-start | bytes 393224 | tf_op jit(solution)/shard_map/while/body/eval_jaxpr/while/body/eval_jaxpr/ppermute | solution.py:19
  462.0 9.7 %all-to-all-start = ((f32[8,1,2]{2,1,0:T(1,128)}), f32[8,1,2]{2,1,0:T(1,128)S(1)}, u32[]{:S(2)}, u32[]{:S(2)}) async-start(f32[8,1,2]{2,1,0:T(1,128)} %broadcast_in_dim.203), calls=%async_computation | async-start | bytes 8192 | tf_op jit(solution)/shard_map/all_to_all | solution.py:24
  466.8 25.9 %copy-start.20 = (f32[1,16,64,128]{3,2,1,0:T(8,128)S(1)}, f32[1,16,64,128]{3,2,1,0:T(8,128)}, u32[]{:S(2)}) copy-start(f32[1,16,64,128]{3,2,1,0:T(8,128)} %get-tuple-element.916) | copy-start | bytes 1572868
  471.7 29.4 %copy-start.58 = (f32[2]{0:T(128)}, f32[2]{0:T(128)S(1)}, u32[]{:S(2)}) copy-start(f32[2]{0:T(128)S(1)} %reduce_sum.33) | copy-start | bytes 28
  472.4 28.2 %all-to-all-start.1 = ((f32[32,1,2]{2,1,0:T(1,128)}), f32[32,1,2]{2,1,0:T(1,128)S(1)}, u32[]{:S(2)}, u32[]{:S(2)}) async-start(f32[32,1,2]{2,1,0:T(1,128)} %broadcast_in_dim.204), calls=%async_computation.1 | async-start | bytes 32768 | tf_op jit(solution)/shard_map/all_to_all | solution.py:24
  (376 other events, 1575.1 us)
where the time goes:
time: 507 us; the launch traced here: 501 us
  local copies, waits for them, and re-layouts  237 us (47%)
  other arithmetic  157 us (31%)
  starting transfers between devices  57.8 us (11%)
  waiting for transfers between devices  35 us (7%)
  loops' own time  9.86 us (2%)
    slice x280, local copies, waits for them, and re-layouts, roll_couple(): return tuple((jnp.roll(values, amount, axis=along) for values in couple))  160 us
    add x60, other arithmetic, relax(): retain * couple[1] + factor * change[1]  70.6 us
    add x60, other arithmetic, relax(): retain * couple[0] + factor * change[0]  54.1 us
    ppermute x20, starting transfers between devices, shifted_2(): return lax.ppermute(value, axis, pairs)  34.3 us
    ppermute x20, waiting for transfers between devices, shifted_2(): return lax.ppermute(value, axis, pairs)  27 us
    all_to_all x2, starting transfers between devices, sent_to_all(): return lax.all_to_all(copies, axis, split_axis=0, concat_axis=0, tiled=True)  23.5 us
    dynamic_slice x10, local copies, waits for them, and re-layouts, snapshot(): waveform[index * INTERVAL + inner]  14.1 us
    while x8, local copies, waits for them, and re-layouts, snapshot(): lax.fori_loop(0, INTERVAL, lambda inner, held: advance(held, waveform[ind...  11.1 us
  transfers between devices with their start and end apart: 22, of which 12 were waited for; matrix products, arithmetic and copies ran while one was open for 44% of the time, Pallas kernels for 0%

commit v1 on v0

v1 whole, which is shorter than its diff:
```python
import functools

import jax
import jax.numpy as jnp
from jax import lax
from jax.experimental import pallas as pl
from jax.experimental.pallas import tpu as pltpu
from jax.sharding import PartitionSpec as P

PML = 16
INTERVAL = 5
NSNAP = 2
MPHASE = 64
NMAT = 3
TIME_STEP = 0.5

MESH = pl.DeviceIdType.MESH
F32 = jnp.float32
TILE = 8
CHUNK = 8


def sent_to_all(shard, axis):
    copies = jnp.broadcast_to(shard, (lax.axis_size(axis), *shard.shape))
    return lax.all_to_all(copies, axis, split_axis=0, concat_axis=0, tiled=True)


def of_everyone(shard, axis):
    return sent_to_all(shard, axis).sum(axis=0)


def kernel(
    slabs,
    rows,
    width,
    depth,
    trig,
    permittivity,
    absorption_peak,
    waveform,
    sheet_in,
    material,
    e_in,
    h_in,
    e_out,
    h_out,
    power_out,
    ef,
    hf,
    e_low,
    h_low,
    mat,
    keep,
    gain,
    sheet,
    e_from,
    h_from,
    load_sem,
    store_sem,
    e_send,
    e_recv,
    h_send,
    h_recv,
):
    ka = lax.axis_index("ka")
    sp = lax.axis_index("sp")
    up = lax.rem(sp + 1, slabs)
    down = lax.rem(sp + slabs - 1, slabs)
    chunks = width // CHUNK
    tiles = width // TILE
    last = rows - 1
    steps = NSNAP * INTERVAL

    first_load = pltpu.make_async_copy(
        e_in.at[0, pl.ds(2, 4), pl.ds(0, 1)], e_low.at[pl.ds(2, 4), pl.ds(0, 1)], load_sem.at[0]
    )
    loads = [
        first_load,
        pltpu.make_async_copy(
            e_in.at[0, pl.ds(0, 2), pl.ds(0, 1)],
            e_low.at[pl.ds(0, 2), pl.ds(0, 1)],
            load_sem.at[1],
        ),
        pltpu.make_async_copy(
            e_in.at[0, :, pl.ds(1, last)], e_low.at[:, pl.ds(1, last)], load_sem.at[2]
        ),
        pltpu.make_async_copy(h_in.at[0], h_low, load_sem.at[3]),
        pltpu.make_async_copy(material, mat, load_sem.at[4]),
    ]
    for load in loads:
        load.start()

    barrier = pltpu.get_barrier_semaphore()
    for other in (up, down):
        pl.semaphore_signal(barrier, inc=1, device_id=(ka, other), device_id_type=MESH)

    def e_copy(chunk):
        where = pl.ds(pl.multiple_of(chunk * CHUNK, CHUNK), CHUNK)
        return pltpu.make_async_remote_copy(
            src_ref=ef.at[pl.ds(2, 4), 0, where],
            dst_ref=e_from.at[:, where],
            send_sem=e_send.at[chunk],
            recv_sem=e_recv.at[chunk],
            device_id=(ka, down),
            device_id_type=MESH,
        )

    def h_copy(chunk):
        begin = pl.multiple_of(chunk * CHUNK, CHUNK)
        return pltpu.make_async_remote_copy(
            src_ref=hf.at[pl.ds(2, 4), last, pl.ds(begin + TILE, CHUNK)],
            dst_ref=h_from.at[:, pl.ds(begin, CHUNK)],
            send_sem=h_send.at[chunk],
            recv_sem=h_recv.at[chunk],
            device_id=(ka, up),
            device_id_type=MESH,
        )

    cos_x, sin_x, cos_y, sin_y = trig[0], trig[1], trig[2], trig[3]
    at_end = sp == slabs - 1
    at_start = sp == 0
    end_cos = jnp.where(at_end, cos_x, 1.0)
    end_sin = jnp.where(at_end, sin_x, 0.0)
    start_cos = jnp.where(at_start, cos_x, 1.0)
    start_sin = jnp.where(at_start, -sin_x, 0.0)

    lane = lax.broadcasted_iota(jnp.int32, (TILE, depth), 1)
    at_top = lane == depth - 1
    at_bottom = lane == 0

    def z_above(values):
        return jnp.where(at_top, 0.0, pltpu.roll(values, depth - 1, 1))

    def z_below(values):
        return jnp.where(at_bottom, 0.0, pltpu.roll(values, 1, 1))

    height = lane.astype(F32)
    low_depth = jnp.maximum(PML - height, 0.0) / PML
    high_depth = jnp.maximum(height - (depth - 1 - PML), 0.0) / PML
    conduct = absorption_peak[0] * (low_depth**3 + high_depth**3)
    half_mag = conduct * (0.5 * TIME_STEP)
    h_keep = (1.0 - half_mag) / (1.0 + half_mag)
    h_gain = -TIME_STEP / (1.0 + half_mag)

    first_load.wait()
    for part in range(2, 6):
        ef[part, 0, pl.ds(0, width), :] = e_low[part, 0].astype(F32)
    pl.semaphore_wait(barrier, 2)
    for chunk in range(chunks):
        e_copy(chunk).start()

    def fill_e_edge(x):
        for part in (0, 4):
            real = ef[part, x, pl.ds(0, 1), :]
            imag = ef[part + 1, x, pl.ds(0, 1), :]
            ef[part, x, pl.ds(width, 1), :] = real * cos_y - imag * sin_y
            ef[part + 1, x, pl.ds(width, 1), :] = real * sin_y + imag * cos_y

    def fill_h_edge(x):
        for part in (0, 4):
            real = hf[part, x, pl.ds(width + TILE - 1, 1), :]
            imag = hf[part + 1, x, pl.ds(width + TILE - 1, 1), :]
            hf[part, x, pl.ds(TILE - 1, 1), :] = real * cos_y + imag * sin_y
            hf[part + 1, x, pl.ds(TILE - 1, 1), :] = imag * cos_y - real * sin_y

    for load in loads[1:]:
        load.wait()
    for part in range(2):
        ef[part, 0, pl.ds(0, width), :] = e_low[part, 0].astype(F32)

    def widen_e(x, carry):
        for part in range(6):
            ef[part, x, pl.ds(0, width), :] = e_low[part, x].astype(F32)
        fill_e_edge(x)
        return carry

    def widen_h(x, carry):
        for part in range(6):
            hf[part, x, pl.ds(TILE, width), :] = h_low[part, x].astype(F32)
        return carry

    fill_e_edge(0)
    lax.fori_loop(1, rows, widen_e, 0)
    lax.fori_loop(0, rows, widen_h, 0)

    keeps = []
    gains = []
    for level in range(NMAT):
        relative = permittivity[level]
        half_ele = conduct * (0.5 * TIME_STEP) / relative
        keeps.append((1.0 - half_ele) / (1.0 + half_ele))
        gains.append(TIME_STEP / jnp.full((TILE, depth), relative, F32) / (1.0 + half_ele))

    def fill_coefficients(x, carry):
        for tile in range(tiles):
            where = pl.ds(tile * TILE, TILE)
            kind = mat[x, where, :]
            keep[x, where, :] = jnp.where(
                kind == 0, keeps[0], jnp.where(kind == 1, keeps[1], keeps[2])
            )
            gain[x, where, :] = jnp.where(
                kind == 0, gains[0], jnp.where(kind == 1, gains[1], gains[2])
            )
        return carry

    lax.fori_loop(0, rows, fill_coefficients, 0)

    at_sheet = lax.broadcasted_iota(jnp.int32, (width, depth), 1) == PML + 2
    for part in range(2):
        turned = sheet_in[0, part].T
        for x in range(rows):
            spread = jnp.broadcast_to(turned[:, x : x + 1], (width, depth))
            sheet[part, x] = jnp.where(at_sheet, spread, 0.0)

    def h_x(part, x, begin):
        ey = ef[2 + part, x, pl.ds(begin, TILE), :]
        ez = ef[4 + part, x, pl.ds(begin, TILE), :]
        ez_y = ef[4 + part, x, pl.ds(begin + 1, TILE), :]
        change = (ez_y - ez) - (z_above(ey) - ey)
        where = pl.ds(begin + TILE, TILE)
        hf[part, x, where, :] = h_keep * hf[part, x, where, :] + h_gain * change

    def h_yz(part, x, begin, ey_x, ez_x):
        ex = ef[part, x, pl.ds(begin, TILE), :]
        ex_y = ef[part, x, pl.ds(begin + 1, TILE), :]
        ey = ef[2 + part, x, pl.ds(begin, TILE), :]
        ez = ef[4 + part, x, pl.ds(begin, TILE), :]
        where = pl.ds(begin + TILE, TILE)
        change_y = (z_above(ex) - ex) - (ez_x - ez)
        change_z = (ey_x - ey) - (ex_y - ex)
        hf[2 + part, x, where, :] = h_keep * hf[2 + part, x, where, :] + h_gain * change_y
        hf[4 + part, x, where, :] = h_keep * hf[4 + part, x, where, :] + h_gain * change_z

    def e_x(part, x, begin, drive):
        where = pl.ds(begin, TILE)
        hy = hf[2 + part, x, pl.ds(begin + TILE, TILE), :]
        hz = hf[4 + part, x, pl.ds(begin + TILE, TILE), :]
        hz_y = hf[4 + part, x, pl.ds(begin + TILE - 1, TILE), :]
        change = (hz - hz_y) - (hy - z_below(hy)) - drive * sheet[part, x, where, :]
        ef[part, x, where, :] = (
            keep[x, where, :] * ef[part, x, where, :] + gain[x, where, :] * change
        )

    def e_yz(part, x, begin, hy_x, hz_x):
        where = pl.ds(begin, TILE)
        hx = hf[part, x, pl.ds(begin + TILE, TILE), :]
        hx_y = hf[part, x, pl.ds(begin + TILE - 1, TILE), :]
        hy = hf[2 + part, x, pl.ds(begin + TILE, TILE), :]
        hz = hf[4 + part, x, pl.ds(begin + TILE, TILE), :]
        change_y = (hx - z_below(hx)) - (hz - hz_x)
        change_z = (hy - hy_x) - (hx - hx_y)
        retain = keep[x, where, :]
        factor = gain[x, where, :]
        ef[2 + part, x, where, :] = retain * ef[2 + part, x, where, :] + factor * change_y
        ef[4 + part, x, where, :] = retain * ef[4 + part, x, where, :] + factor * change_z

    def turned_pair(source, part, where, cosine, sine):
        real = source[part, where, :]
        imag = source[part + 1, where, :]
        return (real * cosine - imag * sine, real * sine + imag * cosine)

    def h_boundary(chunk, carry):
        e_copy(chunk).wait()
        for tile in range(CHUNK // TILE):
            begin = pl.multiple_of(chunk * CHUNK + tile * TILE, TILE)
            ey_x = turned_pair(e_from, 0, pl.ds(begin, TILE), end_cos, end_sin)
            ez_x = turned_pair(e_from, 2, pl.ds(begin, TILE), end_cos, end_sin)
            for part in range(2):
                h_yz(part, last, begin, ey_x[part], ez_x[part])
        h_copy(chunk).start()
        return carry

    def h_row(x, carry):
        for tile in range(tiles):
            begin = tile * TILE
            where = pl.ds(begin, TILE)
            for part in range(2):
                h_x(part, x, begin)
                h_yz(
                    part,
                    x,
                    begin,
                    ef[2 + part, x + 1, where, :],
                    ef[4 + part, x + 1, where, :],
                )
        fill_h_edge(x)
        return carry

    def e_row(drive, x, carry):
        for tile in range(tiles):
            begin = tile * TILE
            where = pl.ds(begin + TILE, TILE)
            for part in range(2):
                e_x(part, x, begin, drive)
                e_yz(
                    part,
                    x,
                    begin,
                    hf[2 + part, x - 1, where, :],
                    hf[4 + part, x - 1, where, :],
                )
        fill_e_edge(x)
        return carry

    def e_boundary(step, chunk, carry):
        h_copy(chunk).wait()
        for tile in range(CHUNK // TILE):
            begin = pl.multiple_of(chunk * CHUNK + tile * TILE, TILE)
            hy_x = turned_pair(h_from, 0, pl.ds(begin, TILE), start_cos, start_sin)
            hz_x = turned_pair(h_from, 2, pl.ds(begin, TILE), start_cos, start_sin)
            for part in range(2):
                e_yz(part, 0, begin, hy_x[part], hz_x[part])

        @pl.when(step < steps - 1)
        def _():
            e_copy(chunk).start()

        return carry

    h_store = pltpu.make_async_copy(hf.at[:, :, pl.ds(TILE, width)], h_out.at[0], store_sem.at[0])
    e_store = pltpu.make_async_copy(ef.at[:, :, pl.ds(0, width)], e_out.at[0], store_sem.at[1])

    def advance(step, carry):
        drive = waveform[step]
        lax.fori_loop(0, chunks, h_boundary, 0)
        for tile in range(tiles):
            for part in range(2):
                h_x(part, last, tile * TILE)
        fill_h_edge(last)
        lax.fori_loop(0, last, h_row, 0)

        @pl.when(step == steps - 1)
        def _():
            h_store.start()

        lax.fori_loop(0, chunks, functools.partial(e_boundary, step), 0)
        for tile in range(tiles):
            for part in range(2):
                e_x(part, 0, tile * TILE, drive)
        fill_e_edge(0)
        lax.fori_loop(1, rows, functools.partial(e_row, drive), 0)
        return carry

    for snap in range(NSNAP):
        lax.fori_loop(snap * INTERVAL, (snap + 1) * INTERVAL, advance, 0)
        if snap == NSNAP - 1:
            e_store.start()

        def add_power(x, total):
            for part in range(4):
                for tile in range(tiles):
                    values = ef[part, x, pl.ds(tile * TILE, TILE), :]
                    total = total + values * values
            return total

        total = lax.fori_loop(0, rows, add_power, jnp.zeros((TILE, depth), F32))
        power_out[snap] = jnp.where(lane == PML + 6, total, 0.0)

    e_store.wait()
    h_store.wait()


def on_device(
    bloch_index,
    material,
    permittivity,
    absorption_peak,
    source_sheet,
    waveform,
    electric_in,
    magnetic_in,
):
    rows, width, depth = material.shape
    slabs = lax.axis_size("sp")
    angles = 2.0 * jnp.pi * bloch_index.astype(F32) / MPHASE
    trig = jnp.stack([jnp.cos(angles[0]), jnp.sin(angles[0])], 1).reshape(4)
    smem = pl.BlockSpec(memory_space=pltpu.SMEM)
    vmem = pl.BlockSpec(memory_space=pltpu.VMEM)
    hbm = pl.BlockSpec(memory_space=pl.ANY)
    chunks = width // CHUNK
    pair = pltpu.SemaphoreType.DMA((chunks,))
    electric_out, magnetic_out, power = pl.pallas_call(
        functools.partial(kernel, slabs, rows, width, depth),
        out_shape=(
            jax.ShapeDtypeStruct(electric_in.shape, F32),
            jax.ShapeDtypeStruct(magnetic_in.shape, F32),
            jax.ShapeDtypeStruct((NSNAP, TILE, depth), F32),
        ),
        in_specs=[smem, smem, smem, smem, vmem, hbm, hbm, hbm],
        out_specs=(hbm, hbm, vmem),
        scratch_shapes=[
            pltpu.VMEM((6, rows, width + TILE, depth), F32),
            pltpu.VMEM((6, rows, width + TILE, depth), F32),
            pltpu.VMEM((6, rows, width, depth), jnp.bfloat16),
            pltpu.VMEM((6, rows, width, depth), jnp.bfloat16),
            pltpu.VMEM((rows, width, depth), jnp.int32),
            pltpu.VMEM((rows, width, depth), F32),
            pltpu.VMEM((rows, width, depth), F32),
            pltpu.VMEM((2, rows, width, depth), F32),
            pltpu.VMEM((4, width, depth), F32),
            pltpu.VMEM((4, width, depth), F32),
            pltpu.SemaphoreType.DMA((5,)),
            pltpu.SemaphoreType.DMA((2,)),
            pair,
            pair,
            pair,
            pair,
        ],
        compiler_params=pltpu.CompilerParams(
            collective_id=0, has_side_effects=True, vmem_limit_bytes=40 * 2**20
        ),
        name="yee",
    )(
        trig,
        permittivity,
        absorption_peak,
        waveform,
        source_sheet,
        material,
        electric_in,
        magnetic_in,
    )
    cells_plane = rows * slabs * width
    reports = (jnp.sum(power, (1, 2)) / cells_plane)[None]
    reflected = of_everyone(reports, "sp")
    total_points = lax.axis_size("ka")
    reflected_mean = of_everyone(jnp.sum(reflected, 0) / total_points, "ka")
    return (electric_out, magnetic_out, reflected, reflected_mean)


def solution(mesh):
    in_specs = (
        P("ka", None),
        P("sp", None, None),
        P(),
        P(),
        P("ka", None, "sp", None),
        P(),
        P("ka", None, "sp", None, None),
        P("ka", None, "sp", None, None),
    )
    out_specs = (
        P("ka", None, "sp", None, None),
        P("ka", None, "sp", None, None),
        P("ka", None),
        P(),
    )
    return jax.shard_map(
        on_device, mesh=mesh, in_specs=in_specs, out_specs=out_specs, check_vma=False
    )
```

time: 507 us -> 151 us (0.30); the launches traced: 501 us -> 150 us
  local copies, waits for them, and re-layouts: 237 us -> 14 us
  other arithmetic: 157 us -> 1.4 us
  Pallas kernels: 0 us -> 90.7 us
  starting transfers between devices: 57.8 us -> 26.2 us
  waiting for transfers between devices: 35 us -> 7.81 us
  loops' own time: 9.86 us -> 0 us
  blocking collectives: 0 us -> 9.02 us
    slice x362 -> x0, local copies, waits for them, and re-layouts: 185 us -> none  [the longest x280 160 us: roll_couple(): return tuple((jnp.roll(values, amount, axis=along) for values in couple))]
    add x120 -> x0, other arithmetic: 125 us -> none  [the longest x60 70.6 us: relax(): retain * couple[1] + factor * change[1]]
    pallas_call x0 -> x1, Pallas kernels: none -> 90.7 us  [on_device(): pl.pallas_call(functools.partial(kernel, slabs, rows, width, depth), out_...]
    ppermute x20 -> x0, starting transfers between devices: 34.3 us -> none  [shifted_2(): return lax.ppermute(value, axis, pairs)]
    ppermute x20 -> x0, waiting for transfers between devices: 27 us -> none  [shifted_2(): return lax.ppermute(value, axis, pairs)]
    while x820 -> x0, local copies, waits for them, and re-layouts: 21 us -> none  [the longest x8 11.1 us: snapshot(): lax.fori_loop(0, INTERVAL, lambda inner, held: advance(held, waveform[ind...]
    dynamic_slice x12 -> x0, local copies, waits for them, and re-layouts: 16.5 us -> none  [the longest x10 14.1 us: snapshot(): waveform[index * INTERVAL + inner]]
    eq x60 -> x0, other arithmetic: 15.3 us -> none  [the longest x10 5.26 us: below_cell(): first = position(couple[0], along) == 0]
  transfers between devices with their start and end apart: 22 -> 1, of which waited for: 12 -> 1; matrix products, arithmetic and copies ran while one was open for 44% -> 0% of each run, Pallas kernels for 0% -> 0%
where the time goes in v1:
time: 151 us; the launch traced here: 150 us
  Pallas kernels  90.7 us (60%)
  starting transfers between devices  26.2 us (17%)
  local copies, waits for them, and re-layouts  14 us (9%)
  blocking collectives  9.02 us (6%)
  waiting for transfers between devices  7.81 us (5%)
    pallas_call x1, Pallas kernels, on_device(): pl.pallas_call(functools.partial(kernel, slabs, rows, width, depth), out_...  90.7 us
    all_to_all x1, starting transfers between devices, sent_to_all(): return lax.all_to_all(copies, axis, split_axis=0, concat_axis=0, tiled=True)  26.2 us
    unnamed x18, local copies, waits for them, and re-layouts  13.2 us
    all_to_all x1, blocking collectives, sent_to_all(): return lax.all_to_all(copies, axis, split_axis=0, concat_axis=0, tiled=True)  9.02 us
    all_to_all x1, waiting for transfers between devices, sent_to_all(): return lax.all_to_all(copies, axis, split_axis=0, concat_axis=0, tiled=True)  7.81 us
  transfers between devices with their start and end apart: 1, of which 1 were waited for; matrix products, arithmetic and copies ran while one was open for 0% of the time, Pallas kernels for 0%

profile of v1, /device:TPU:1, one launch (start us, length us, event | category | flops | bytes accessed | tf_op | source)
XLA Modules:
  0.0 150.4 jit_solution(8507277334250932976)
XLA Ops:
  0.6 0.7 cosine_bitcast_fusion
  1.3 0.1 copy.14
  1.4 0.1 reshape.40.trig
  2.2 0.0 copy-start.1
  2.2 1.4 copy-done.1
  3.6 0.0 copy-start.2
  3.6 1.4 copy-done.2
  5.0 0.0 copy-start.3
  5.0 1.0 copy-done.3
  6.0 0.0 copy-start.4
  6.0 0.7 copy-done.4
  6.8 0.0 copy-start.5
  6.8 0.7 copy-done.5
  7.4 0.0 copy-start.6
  7.4 0.7 copy-done.6
  8.1 90.7 %yee.1 = (f32[1,6,16,64,128]{4,3,2,1,0:T(8,128)S(1)}, f32[1,6,16,64,128]{4,3,2,1,0:T(8,128)S(1)}, f32[2,8,128]{2,1,0:T(8,128)S(1)}) custom-call(f32[4]{0:T(128)S(1)} %reshape.40.trig, f32[3]{0:T(128)S(1)} %copy-done.5, f32[1]{0:T(128)S(6)} %copy.21.absorption_peak, f32[10]{0:T(128)S(1)} %copy-done.6, f32[1,2,16,64]{3,2,1,0:T(8,128)S(1)} %copy-done.4, ...), custom_call_target="tpu_custom_call" | custom-call | tf_op jit(solution)/shard_map/yee/pallas_call | solution.py:382
  98.8 0.0 copy-start
  98.8 1.7 %copy-done = f32[1,6,16,64,128]{4,3,2,1,0:T(8,128)} copy-done((f32[1,6,16,64,128]{4,3,2,1,0:T(8,128)}, f32[1,6,16,64,128]{4,3,2,1,0:T(8,128)S(1)}, u32[]{:S(2)}) %copy-start) | copy-done | bytes 3145752
  100.4 0.1 reduce_sum.33
  100.5 9.0 %all_to_all.11 = f32[8,1,2]{2,1,0:T(1,128)S(1)} all-to-all(f32[8,1,2]{2,1,0:T(1,128)S(1)} %broadcast_in_dim.7), channel_id=1, replica_groups=mesh['ka'=32,'sp'=8] {'sp'}, dimensions={0} | all-to-all | bytes 128 | tf_op jit(solution)/shard_map/all_to_all | solution.py:25
  109.6 0.0 copy-start.7
  109.6 0.6 broadcast_in_dim.8
  110.2 26.2 %all-to-all-start.1 = ((f32[32,1,2]{2,1,0:T(1,128)}), f32[32,1,2]{2,1,0:T(1,128)S(1)}, u32[]{:S(2)}, u32[]{:S(2)}) async-start(f32[32,1,2]{2,1,0:T(1,128)} %broadcast_in_dim.8), calls=%async_computation.1 | async-start | bytes 32768 | tf_op jit(solution)/shard_map/all_to_all | solution.py:25
  136.4 7.8 %all-to-all-done.1 = f32[32,1,2]{2,1,0:T(1,128)S(1)} async-done(((f32[32,1,2]{2,1,0:T(1,128)}), f32[32,1,2]{2,1,0:T(1,128)S(1)}, u32[]{:S(2)}, u32[]{:S(2)}) %all-to-all-start.1) | async-done | bytes 288 | tf_op jit(solution)/shard_map/all_to_all | solution.py:25
  144.2 0.6 reduce_sum.36
  144.8 4.0 %copy.22 = f32[1,6,16,64,128]{4,3,2,1,0:T(8,128)} copy(f32[1,6,16,64,128]{4,3,2,1,0:T(8,128)} %copy-done) | data formatting | bytes 6291456
  148.7 0.0 copy-done.7
  148.7 1.7 %copy.23 = f32[1,6,16,64,128]{4,3,2,1,0:T(8,128)} copy(f32[1,6,16,64,128]{4,3,2,1,0:T(8,128)S(1)} %get-tuple-element.17) | data formatting | bytes 6291456
  (5 shorter events, 0.1 us)
Async XLA Ops:
  2.2 1.4 copy-start.1
  3.6 1.4 copy-start.2
  5.0 1.0 copy-start.3
  6.0 0.7 copy-start.4
  6.8 0.7 copy-start.5
  7.4 0.7 copy-start.6
  98.8 1.7 %copy-start = (f32[1,6,16,64,128]{4,3,2,1,0:T(8,128)}, f32[1,6,16,64,128]{4,3,2,1,0:T(8,128)S(1)}, u32[]{:S(2)}) copy-start(f32[1,6,16,64,128]{4,3,2,1,0:T(8,128)S(1)} %get-tuple-element.16) | copy-start | bytes 9437188
  109.6 39.1 %copy-start.7 = (f32[2]{0:T(128)}, f32[2]{0:T(128)S(1)}, u32[]{:S(2)}) copy-start(f32[2]{0:T(128)S(1)} %reduce_sum.34) | copy-start | bytes 28
  110.2 34.0 %all-to-all-start.1 = ((f32[32,1,2]{2,1,0:T(1,128)}), f32[32,1,2]{2,1,0:T(1,128)S(1)}, u32[]{:S(2)}, u32[]{:S(2)}) async-start(f32[32,1,2]{2,1,0:T(1,128)} %broadcast_in_dim.8), calls=%async_computation.1 | async-start | bytes 32768 | tf_op jit(solution)/shard_map/all_to_all | solution.py:25

commit v2 on v1

v2 whole, which is shorter than its diff:
```python
import functools

import jax
import jax.numpy as jnp
from jax import lax
from jax.experimental import pallas as pl
from jax.experimental.pallas import tpu as pltpu
from jax.sharding import PartitionSpec as P

PML = 16
INTERVAL = 5
NSNAP = 2
MPHASE = 64
NMAT = 3
TIME_STEP = 0.5

MESH = pl.DeviceIdType.MESH
F32 = jnp.float32
TILE = 8


def kernel(
    sizes,
    bloch,
    permittivity,
    absorption_peak,
    waveform,
    sheet_in,
    material,
    e_in,
    h_in,
    e_out,
    h_out,
    reflected_out,
    mean_out,
    ef,
    hf,
    e_low,
    h_low,
    mat,
    keep,
    gain,
    sheet_raw,
    sheet,
    from_up,
    from_down,
    ghost_h,
    ghost_ex,
    ghost_kind,
    ghost_raw,
    ghost_keep,
    ghost_gain,
    ghost_sheet,
    my_kind,
    totals,
    slab_sums,
    point_sums,
    load_sem,
    up_send,
    up_recv,
    down_send,
    down_recv,
    ghost_send,
    ghost_recv,
    extra_send,
    extra_recv,
    slab_send,
    slab_recv,
    point_send,
    point_recv,
):
    points, slabs, rows, width, depth = sizes
    ka = lax.axis_index("ka")
    sp = lax.axis_index("sp")
    up = lax.rem(sp + 1, slabs)
    down = lax.rem(sp + slabs - 1, slabs)
    tiles = width // TILE
    last = rows - 1
    steps = NSNAP * INTERVAL
    inside = pl.ds(TILE, width)
    whole = pl.ds(0, width)

    barrier = pltpu.get_barrier_semaphore()
    for other in (up, down):
        pl.semaphore_signal(barrier, inc=1, device_id=(ka, other), device_id_type=MESH)

    def greet(offset, carry):
        peer = lax.rem(ka + offset, points)
        pl.semaphore_signal(barrier, inc=1, device_id=(peer, sp), device_id_type=MESH)
        return carry

    def load(source, target, index):
        copy = pltpu.make_async_copy(source, target, load_sem.at[index])
        copy.start()
        return copy

    middle = pl.ds(1, rows - 2)
    load_first = load(e_in.at[0, :, 0], e_low.at[:, 0], 0)
    load_last = load(e_in.at[0, :, last], e_low.at[:, last], 1)
    load_h_last = load(h_in.at[0, :, last], h_low.at[:, last], 2)
    load_mat_last = load(material.at[last], mat.at[last], 3)
    load_sheet = load(sheet_in.at[0], sheet_raw, 4)
    load_e = load(e_in.at[0, :, middle], e_low.at[:, middle], 5)
    load_h = load(h_in.at[0, :, pl.ds(0, last)], h_low.at[:, pl.ds(0, last)], 6)
    load_mat = load(material.at[pl.ds(0, last)], mat.at[pl.ds(0, last)], 7)
    lax.fori_loop(1, points, greet, 0)

    def remote(source, target, send, recv, other):
        return pltpu.make_async_remote_copy(
            src_ref=source,
            dst_ref=target,
            send_sem=send,
            recv_sem=recv,
            device_id=(ka, other),
            device_id_type=MESH,
        )

    def copy_up(slot, chunk):
        where = pl.ds(chunk * TILE, TILE)
        return remote(
            ef.at[pl.ds(2, 4), last, where],
            from_down.at[slot, :, where],
            up_send.at[chunk],
            up_recv.at[slot, chunk],
            up,
        )

    def copy_down(slot, chunk):
        where = pl.ds(chunk * TILE, TILE)
        return remote(
            ef.at[pl.ds(2, 4), 0, where],
            from_up.at[slot, :, where],
            down_send.at[chunk],
            down_recv.at[slot, chunk],
            down,
        )

    def copy_ghost(chunk):
        where = pl.ds((chunk + 1) * TILE, TILE)
        return remote(
            hf.at[pl.ds(2, 4), last, where],
            ghost_h.at[:, where],
            ghost_send.at[chunk],
            ghost_recv.at[chunk],
            up,
        )

    extras = [
        remote(
            ef.at[pl.ds(0, 2), last, whole],
            ghost_ex.at[:, whole],
            extra_send.at[0],
            extra_recv.at[0],
            up,
        ),
        remote(my_kind, ghost_kind, extra_send.at[1], extra_recv.at[1], up),
        remote(
            sheet_raw.at[:, pl.ds(rows - TILE, TILE)],
            ghost_raw,
            extra_send.at[2],
            extra_recv.at[2],
            up,
        ),
    ]

    load_first.wait()
    load_last.wait()
    for part in range(6):
        ef[part, last, whole, :] = e_low[part, last].astype(F32)
    for part in range(6):
        ef[part, 0, whole, :] = e_low[part, 0].astype(F32)
    load_h_last.wait()
    for part in range(6):
        hf[part, last, inside, :] = h_low[part, last].astype(F32)
    load_mat_last.wait()
    my_kind[...] = mat[last].astype(F32)
    load_sheet.wait()
    pl.semaphore_wait(barrier, points + 1)
    extras[0].start()
    for chunk in range(tiles):
        copy_up(0, chunk).start()
        copy_down(0, chunk).start()
        copy_ghost(chunk).start()
    extras[1].start()
    extras[2].start()

    angle_x = jnp.full((1, depth), 2.0 * jnp.pi * bloch[0, 0].astype(F32) / MPHASE, F32)
    angle_y = jnp.full((1, depth), 2.0 * jnp.pi * bloch[0, 1].astype(F32) / MPHASE, F32)
    cos_x, sin_x = jnp.cos(angle_x), jnp.sin(angle_x)
    cos_y, sin_y = jnp.cos(angle_y), jnp.sin(angle_y)
    at_end = sp == slabs - 1
    at_start = sp == 0
    end_cos = jnp.where(at_end, cos_x, 1.0)
    end_sin = jnp.where(at_end, sin_x, 0.0)
    start_cos = jnp.where(at_start, cos_x, 1.0)
    start_sin = jnp.where(at_start, -sin_x, 0.0)

    lane = lax.broadcasted_iota(jnp.int32, (TILE, depth), 1)
    at_top = lane == depth - 1
    at_bottom = lane == 0

    def z_above(values):
        return jnp.where(at_top, 0.0, pltpu.roll(values, depth - 1, 1))

    def z_below(values):
        return jnp.where(at_bottom, 0.0, pltpu.roll(values, 1, 1))

    height = lane.astype(F32)
    low_depth = jnp.maximum(PML - height, 0.0) / PML
    high_depth = jnp.maximum(height - (depth - 1 - PML), 0.0) / PML
    conduct = absorption_peak[0] * (low_depth**3 + high_depth**3)
    half_mag = conduct * (0.5 * TIME_STEP)
    h_keep = (1.0 - half_mag) / (1.0 + half_mag)
    h_gain = -TIME_STEP / (1.0 + half_mag)

    def rotate(pair, cosine, sine):
        return (pair[0] * cosine - pair[1] * sine, pair[0] * sine + pair[1] * cosine)

    def upper_edge(refs):
        first, edge = pl.ds(0, 1), pl.ds(width, 1)
        real, imag = rotate((refs[0][first, :], refs[1][first, :]), cos_y, sin_y)
        refs[0][edge, :] = real
        refs[1][edge, :] = imag

    def lower_edge(refs):
        end, edge = pl.ds(width + TILE - 1, 1), pl.ds(TILE - 1, 1)
        real, imag = rotate((refs[0][end, :], refs[1][end, :]), cos_y, -sin_y)
        refs[0][edge, :] = real
        refs[1][edge, :] = imag

    def fill_e_edge(x):
        for part in (0, 4):
            upper_edge((ef.at[part, x], ef.at[part + 1, x]))

    def fill_h_edge(x, parts=(0, 4)):
        for part in parts:
            lower_edge((hf.at[part, x], hf.at[part + 1, x]))

    def fill_ghost_ex_edge():
        upper_edge((ghost_ex.at[0], ghost_ex.at[1]))

    def fill_ghost_h_edge():
        lower_edge((ghost_h.at[2], ghost_h.at[3]))

    keeps = []
    gains = []
    for level in range(NMAT):
        relative = jnp.full((TILE, depth), permittivity[level], F32)
        half_ele = conduct * (0.5 * TIME_STEP) / relative
        keeps.append((1.0 - half_ele) / (1.0 + half_ele))
        gains.append(TIME_STEP / relative / (1.0 + half_ele))

    def choose(kind, table, zero, one):
        return jnp.where(kind == zero, table[0], jnp.where(kind == one, table[1], table[2]))

    load_e.wait()
    load_h.wait()
    load_mat.wait()

    def widen_e(x, carry):
        for part in range(6):
            ef[part, x, whole, :] = e_low[part, x].astype(F32)
        fill_e_edge(x)
        return carry

    def widen_h(x, carry):
        for part in range(6):
            hf[part, x, inside, :] = h_low[part, x].astype(F32)
        return carry

    def fill_coefficients(x, carry):
        for tile in range(tiles):
            where = pl.ds(tile * TILE, TILE)
            kind = mat[x, where, :]
            keep[x, where, :] = choose(kind, keeps, 0, 1)
            gain[x, where, :] = choose(kind, gains, 0, 1)
        return carry

    fill_e_edge(0)
    fill_e_edge(last)
    lax.fori_loop(1, last, widen_e, 0)
    lax.fori_loop(0, last, widen_h, 0)
    lax.fori_loop(0, rows, fill_coefficients, 0)

    at_sheet = lax.broadcasted_iota(jnp.int32, (width, depth), 1) == PML + 2
    for part in range(2):
        turned = sheet_raw[part].T
        for x in range(rows):
            spread = jnp.broadcast_to(turned[:, x : x + 1], (width, depth))
            sheet[part, x] = jnp.where(at_sheet, spread, 0.0)

    def h_x(part, x, begin):
        ey = ef[2 + part, x, pl.ds(begin, TILE), :]
        ez = ef[4 + part, x, pl.ds(begin, TILE), :]
        ez_y = ef[4 + part, x, pl.ds(begin + 1, TILE), :]
        change = (ez_y - ez) - (z_above(ey) - ey)
        where = pl.ds(begin + TILE, TILE)
        hf[part, x, where, :] = h_keep * hf[part, x, where, :] + h_gain * change

    def h_yz(part, x, begin, ey_x, ez_x):
        ex = ef[part, x, pl.ds(begin, TILE), :]
        ex_y = ef[part, x, pl.ds(begin + 1, TILE), :]
        ey = ef[2 + part, x, pl.ds(begin, TILE), :]
        ez = ef[4 + part, x, pl.ds(begin, TILE), :]
        where = pl.ds(begin + TILE, TILE)
        change_y = (z_above(ex) - ex) - (ez_x - ez)
        change_z = (ey_x - ey) - (ex_y - ex)
        hf[2 + part, x, where, :] = h_keep * hf[2 + part, x, where, :] + h_gain * change_y
        hf[4 + part, x, where, :] = h_keep * hf[4 + part, x, where, :] + h_gain * change_z

    def ghost_h_yz(part, begin, ey, ez):
        ex = ghost_ex[part, pl.ds(begin, TILE), :]
        ex_y = ghost_ex[part, pl.ds(begin + 1, TILE), :]
        ey_x = ef[2 + part, 0, pl.ds(begin, TILE), :]
        ez_x = ef[4 + part, 0, pl.ds(begin, TILE), :]
        where = pl.ds(begin + TILE, TILE)
        change_y = (z_above(ex) - ex) - (ez_x - ez)
        change_z = (ey_x - ey) - (ex_y - ex)
        ghost_h[part, where, :] = h_keep * ghost_h[part, where, :] + h_gain * change_y
        ghost_h[2 + part, where, :] = h_keep * ghost_h[2 + part, where, :] + h_gain * change_z

    def e_x(part, x, begin, drive):
        where = pl.ds(begin, TILE)
        hy = hf[2 + part, x, pl.ds(begin + TILE, TILE), :]
        hz = hf[4 + part, x, pl.ds(begin + TILE, TILE), :]
        hz_y = hf[4 + part, x, pl.ds(begin + TILE - 1, TILE), :]
        change = (hz - hz_y) - (hy - z_below(hy)) - drive * sheet[part, x, where, :]
        ef[part, x, where, :] = (
            keep[x, where, :] * ef[part, x, where, :] + gain[x, where, :] * change
        )

    def ghost_e_x(part, begin, drive):
        where = pl.ds(begin, TILE)
        hy = ghost_h[part, pl.ds(begin + TILE, TILE), :]
        hz = ghost_h[2 + part, pl.ds(begin + TILE, TILE), :]
        hz_y = ghost_h[2 + part, pl.ds(begin + TILE - 1, TILE), :]
        change = (hz - hz_y) - (hy - z_below(hy)) - drive * ghost_sheet[part, where, :]
        ghost_ex[part, where, :] = (
            ghost_keep[where, :] * ghost_ex[part, where, :] + ghost_gain[where, :] * change
        )

    def e_yz(part, x, begin, hy_x, hz_x):
        where = pl.ds(begin, TILE)
        hx = hf[part, x, pl.ds(begin + TILE, TILE), :]
        hx_y = hf[part, x, pl.ds(begin + TILE - 1, TILE), :]
        hy = hf[2 + part, x, pl.ds(begin + TILE, TILE), :]
        hz = hf[4 + part, x, pl.ds(begin + TILE, TILE), :]
        change_y = (hx - z_below(hx)) - (hz - hz_x)
        change_z = (hy - hy_x) - (hx - hx_y)
        retain = keep[x, where, :]
        factor = gain[x, where, :]
        ef[2 + part, x, where, :] = retain * ef[2 + part, x, where, :] + factor * change_y
        ef[4 + part, x, where, :] = retain * ef[4 + part, x, where, :] + factor * change_z

    def h_row(x, carry):
        for tile in range(tiles):
            begin = tile * TILE
            where = pl.ds(begin, TILE)
            for part in range(2):
                h_x(part, x, begin)
                h_yz(
                    part, x, begin, ef[2 + part, x + 1, where, :], ef[4 + part, x + 1, where, :]
                )
        fill_h_edge(x)
        return carry

    def h_row_out(x, carry):
        h_row(x, carry)
        for part in range(6):
            h_out[0, part, x] = hf[part, x, inside, :]
        return carry

    def e_row(drive, x, carry):
        for tile in range(tiles):
            begin = tile * TILE
            where = pl.ds(begin + TILE, TILE)
            for part in range(2):
                e_x(part, x, begin, drive)
                e_yz(
                    part, x, begin, hf[2 + part, x - 1, where, :], hf[4 + part, x - 1, where, :]
                )
        fill_e_edge(x)
        return carry

    def add_power(index, x):
        total = totals[index]
        for part in range(4):
            for tile in range(tiles):
                values = ef[part, x, pl.ds(tile * TILE, TILE), :]
                total = total + values * values
        totals[index] = total

    def e_row_out(drive, x, carry):
        e_row(drive, x, carry)
        for part in range(6):
            e_out[0, part, x] = ef[part, x, whole, :]
        add_power(NSNAP - 1, x)
        return carry

    def e_x_ends(drive):
        for x in (0, last):
            for tile in range(tiles):
                for part in range(2):
                    e_x(part, x, tile * TILE, drive)

    def finish_electric(drive):
        fill_h_edge(last, (4,))
        fill_ghost_h_edge()
        for tile in range(tiles):
            for part in range(2):
                ghost_e_x(part, tile * TILE, drive)
        fill_ghost_ex_edge()
        e_x_ends(drive)
        fill_e_edge(0)
        fill_e_edge(last)
        e_row(drive, 1, 0)
        e_row(drive, last - 1, 0)

    def begin_magnetic():
        h_row(0, 0)
        h_row(last - 1, 0)
        for tile in range(tiles):
            for part in range(2):
                h_x(part, last, tile * TILE)
        fill_h_edge(last, (0,))

    def pair_of(ref, part, where):
        return (ref[part, where, :], ref[part + 1, where, :])

    def receive(slot, chunk):
        arriving_up = copy_up(slot, chunk)
        arriving_down = copy_down(slot, chunk)
        arriving_up.wait()
        arriving_down.wait()
        begin = chunk * TILE
        where = pl.ds(begin, TILE)
        ey_up = rotate(pair_of(from_up.at[slot], 0, where), end_cos, end_sin)
        ez_up = rotate(pair_of(from_up.at[slot], 2, where), end_cos, end_sin)
        ey_down = rotate(pair_of(from_down.at[slot], 0, where), start_cos, start_sin)
        ez_down = rotate(pair_of(from_down.at[slot], 2, where), start_cos, start_sin)
        beyond = pl.ds(begin + TILE, TILE)
        for part in range(2):
            h_yz(part, last, begin, ey_up[part], ez_up[part])
            ghost_h_yz(part, begin, ey_down[part], ez_down[part])
        for part in range(2):
            e_yz(part, last, begin, hf[2 + part, last - 1, beyond, :], hf[4 + part, last - 1, beyond, :])
            e_yz(part, 0, begin, ghost_h[part, beyond, :], ghost_h[2 + part, beyond, :])

    def share(first, end, part, pieces):
        count = end - first
        return first + count * part // pieces, first + count * (part + 1) // pieces

    totals[...] = jnp.zeros(totals.shape, F32)

    extras[0].wait()
    real, imag = rotate((ghost_ex[0, whole, :], ghost_ex[1, whole, :]), start_cos, start_sin)
    ghost_ex[0, whole, :] = real
    ghost_ex[1, whole, :] = imag
    fill_ghost_ex_edge()

    def finish_ghost():
        extras[1].wait()
        extras[2].wait()
        for tile in range(tiles):
            where = pl.ds(tile * TILE, TILE)
            kind = ghost_kind[where, :]
            ghost_keep[where, :] = choose(kind, keeps, 0.0, 1.0)
            ghost_gain[where, :] = choose(kind, gains, 0.0, 1.0)
        real, imag = rotate(
            (ghost_raw[0], ghost_raw[1]), start_cos[:, :width], start_sin[:, :width]
        )
        for part, raw in enumerate((real, imag)):
            column = raw.T[:, TILE - 1 : TILE]
            spread = jnp.broadcast_to(column, (width, depth))
            ghost_sheet[part] = jnp.where(at_sheet, spread, 0.0)

    half = tiles // 2

    def advance(step, carry):
        slot = lax.rem(step, 2)
        drive = waveform[jnp.maximum(step - 1, 0)]

        @pl.when(step > 0)
        def _():
            finish_electric(drive)

        @pl.when(step == INTERVAL)
        def _():
            for x in (0, 1, last - 1, last):
                add_power(0, x)

        begin_magnetic()
        for chunk in range(tiles):

            @pl.when(step == 0)
            def _():
                copy_ghost(chunk).wait()
                where = pl.ds((chunk + 1) * TILE, TILE)
                for part in (0, 2):
                    real, imag = rotate(pair_of(ghost_h, part, where), start_cos, start_sin)
                    ghost_h[part, where, :] = real
                    ghost_h[part + 1, where, :] = imag

            receive(slot, chunk)
            copy_up(1 - slot, chunk).start()
            copy_down(1 - slot, chunk).start()
            if chunk < half:

                @pl.when(step > 0)
                def _():
                    begin, end = share(2, last - 1, chunk, half)
                    lax.fori_loop(begin, end, functools.partial(e_row, drive), 0)

            else:
                begin, end = share(1, last - 1, chunk - half, tiles - half)
                lax.fori_loop(begin, end, h_row, 0)

        @pl.when(step == INTERVAL)
        def _():
            def add(x, inner):
                add_power(0, x)
                return inner

            lax.fori_loop(2, last - 1, add, 0)

        @pl.when(step == 0)
        def _():
            finish_ghost()

        return carry

    lax.fori_loop(0, steps - 1, advance, 0)

    slot = (steps - 1) % 2
    drive = waveform[steps - 2]
    finish_electric(drive)
    lax.fori_loop(2, last - 1, functools.partial(e_row, drive), 0)
    begin_magnetic()
    lax.fori_loop(1, last - 1, h_row_out, 0)
    for x in (0, last - 1):
        for part in range(6):
            h_out[0, part, x] = hf[part, x, inside, :]
    final = waveform[steps - 1]
    lax.fori_loop(1, last, functools.partial(e_row_out, final), 0)
    for chunk in range(tiles):
        receive(slot, chunk)
    fill_h_edge(last, (4,))
    e_x_ends(final)
    add_power(NSNAP - 1, 0)
    add_power(NSNAP - 1, last)

    row_index = lax.broadcasted_iota(jnp.int32, (TILE, depth), 0)
    at_monitor = lane == PML + 6
    mine = jnp.zeros((TILE, depth), F32)
    for snap in range(NSNAP):
        mine = jnp.where(row_index == snap, jnp.sum(jnp.where(at_monitor, totals[snap], 0.0)), mine)
    slab_sums[0] = mine

    def slab_copy(offset):
        return remote(
            slab_sums.at[0],
            slab_sums.at[offset],
            slab_send.at[offset],
            slab_recv.at[offset],
            lax.rem(sp + offset, slabs),
        )

    def point_copy(offset):
        return pltpu.make_async_remote_copy(
            src_ref=point_sums.at[0],
            dst_ref=point_sums.at[offset],
            send_sem=point_send.at[offset],
            recv_sem=point_recv.at[offset],
            device_id=(lax.rem(ka + offset, points), sp),
            device_id_type=MESH,
        )

    def started(copy):
        def start(offset, carry):
            copy(offset).start()
            return carry

        return start

    def waited(copy):
        def wait(offset, carry):
            copy(offset).wait()
            return carry

        return wait

    lax.fori_loop(1, slabs, started(slab_copy), 0)
    for x in (0, last):
        for part in range(6):
            e_out[0, part, x] = ef[part, x, whole, :]
    for part in range(6):
        h_out[0, part, last] = hf[part, last, inside, :]
    lax.fori_loop(1, slabs, waited(slab_copy), 0)
    total = slab_sums[0]
    for offset in range(1, slabs):
        total = total + slab_sums[offset]
    total = total / (rows * slabs * width)
    point_sums[0] = total
    reflected_out[...] = total
    lax.fori_loop(1, points, started(point_copy), 0)
    lax.fori_loop(1, points, waited(point_copy), 0)
    total = point_sums[0]
    for offset in range(1, points):
        total = total + point_sums[offset]
    mean_out[...] = total / points


def on_device(
    bloch_index,
    material,
    permittivity,
    absorption_peak,
    source_sheet,
    waveform,
    electric_in,
    magnetic_in,
):
    rows, width, depth = material.shape
    slabs = lax.axis_size("sp")
    points = lax.axis_size("ka")
    tiles = width // TILE
    smem = pl.BlockSpec(memory_space=pltpu.SMEM)
    vmem = pl.BlockSpec(memory_space=pltpu.VMEM)
    hbm = pl.BlockSpec(memory_space=pltpu.HBM)
    dma = pltpu.SemaphoreType.DMA
    tile = jax.ShapeDtypeStruct((TILE, depth), F32)
    electric_out, magnetic_out, reflected, mean = pl.pallas_call(
        functools.partial(kernel, (points, slabs, rows, width, depth)),
        out_shape=(
            jax.ShapeDtypeStruct(electric_in.shape, F32),
            jax.ShapeDtypeStruct(magnetic_in.shape, F32),
            tile,
            tile,
        ),
        in_specs=[smem, smem, smem, smem, hbm, hbm, hbm, hbm],
        out_specs=(vmem, vmem, vmem, vmem),
        scratch_shapes=[
            pltpu.VMEM((6, rows, width + TILE, depth), F32),
            pltpu.VMEM((6, rows, width + TILE, depth), F32),
            pltpu.VMEM((6, rows, width, depth), jnp.bfloat16),
            pltpu.VMEM((6, rows, width, depth), jnp.bfloat16),
            pltpu.VMEM((rows, width, depth), jnp.int32),
            pltpu.VMEM((rows, width, depth), F32),
            pltpu.VMEM((rows, width, depth), F32),
            pltpu.VMEM((2, rows, width), F32),
            pltpu.VMEM((2, rows, width, depth), F32),
            pltpu.VMEM((2, 4, width, depth), F32),
            pltpu.VMEM((2, 4, width, depth), F32),
            pltpu.VMEM((4, width + TILE, depth), F32),
            pltpu.VMEM((2, width + TILE, depth), F32),
            pltpu.VMEM((width, depth), F32),
            pltpu.VMEM((2, TILE, width), F32),
            pltpu.VMEM((width, depth), F32),
            pltpu.VMEM((width, depth), F32),
            pltpu.VMEM((2, width, depth), F32),
            pltpu.VMEM((width, depth), F32),
            pltpu.VMEM((NSNAP, TILE, depth), F32),
            pltpu.VMEM((slabs, TILE, depth), F32),
            pltpu.VMEM((points, TILE, depth), F32),
            dma((8,)),
            dma((tiles,)),
            dma((2, tiles)),
            dma((tiles,)),
            dma((2, tiles)),
            dma((tiles,)),
            dma((tiles,)),
            dma((3,)),
            dma((3,)),
            dma((slabs,)),
            dma((slabs,)),
            dma((points,)),
            dma((points,)),
        ],
        compiler_params=pltpu.CompilerParams(
            collective_id=0, has_side_effects=True, vmem_limit_bytes=32 * 2**20
        ),
        name="yee",
    )(
        bloch_index,
        permittivity,
        absorption_peak,
        waveform,
        source_sheet,
        material,
        electric_in,
        magnetic_in,
    )
    return (electric_out, magnetic_out, reflected[None, :NSNAP, 0], mean[:NSNAP, 0])


def solution(mesh):
    in_specs = (
        P("ka", None),
        P("sp", None, None),
        P(),
        P(),
        P("ka", None, "sp", None),
        P(),
        P("ka", None, "sp", None, None),
        P("ka", None, "sp", None, None),
    )
    out_specs = (
        P("ka", None, "sp", None, None),
        P("ka", None, "sp", None, None),
        P("ka", None),
        P(),
    )
    return jax.shard_map(
        on_device, mesh=mesh, in_specs=in_specs, out_specs=out_specs, check_vma=False
    )
```

time: 151 us -> 101 us (0.67)
  starting transfers between devices: 26.2 us -> 0 us
  blocking collectives: 9.02 us -> 0 us
  waiting for transfers between devices: 7.81 us -> 0 us
  local copies, waits for them, and re-layouts: 14 us -> 10.5 us
    all_to_all x1 -> x0, starting transfers between devices: 26.2 us -> none  [sent_to_all(): return lax.all_to_all(copies, axis, split_axis=0, concat_axis=0, tiled=True)]
    all_to_all x1 -> x0, blocking collectives: 9.02 us -> none  [sent_to_all(): return lax.all_to_all(copies, axis, split_axis=0, concat_axis=0, tiled=True)]
    all_to_all x1 -> x0, waiting for transfers between devices: 7.81 us -> none  [sent_to_all(): return lax.all_to_all(copies, axis, split_axis=0, concat_axis=0, tiled=True)]
    unnamed x18 -> x16, local copies, waits for them, and re-layouts: 13.2 us -> 9.86 us
    pallas_call x1, Pallas kernels: 90.7 us -> 89.2 us  [on_device(): pl.pallas_call(functools.partial(kernel, (points, slabs, rows, width, dep...]
  transfers between devices with their start and end apart: 1 -> 0, of which waited for: 1 -> 0; matrix products, arithmetic and copies ran while one was open for 0% -> 0% of each run, Pallas kernels for 0% -> 0%
where the time goes in v2:
time: 101 us
  Pallas kernels  89.2 us (88%)
  local copies, waits for them, and re-layouts  10.5 us (10%)
  between operations  1.3 us (1%)
    pallas_call x1, Pallas kernels, on_device(): pl.pallas_call(functools.partial(kernel, (points, slabs, rows, width, dep...  89.2 us
    unnamed x16, local copies, waits for them, and re-layouts  9.86 us

profile of v2, /device:TPU:1, one launch (start us, length us, event | category | flops | bytes accessed | tf_op | source)
XLA Modules:
  0.0 101.0 jit_solution(7685839803595147728)
XLA Ops:
  1.3 0.0 copy-start
  1.3 1.4 %copy-done = bf16[1,6,16,64,128]{4,3,2,1,0:T(8,128)(2,1)S(1)} copy-done((bf16[1,6,16,64,128]{4,3,2,1,0:T(8,128)(2,1)S(1)}, bf16[1,6,16,64,128]{4,3,2,1,0:T(8,128)(2,1)}, u32[]{:S(2)}) %copy-start) | copy-done | bytes 1572888
  2.7 0.0 copy-start.1
  2.7 1.4 %copy-done.1 = bf16[1,6,16,64,128]{4,3,2,1,0:T(8,128)(2,1)S(1)} copy-done((bf16[1,6,16,64,128]{4,3,2,1,0:T(8,128)(2,1)S(1)}, bf16[1,6,16,64,128]{4,3,2,1,0:T(8,128)(2,1)}, u32[]{:S(2)}) %copy-start.1) | copy-done | bytes 1572888
  4.1 0.0 copy-start.2
  4.1 1.0 %copy-done.2 = s32[16,64,128]{2,1,0:T(8,128)S(1)} copy-done((s32[16,64,128]{2,1,0:T(8,128)S(1)}, s32[16,64,128]{2,1,0:T(8,128)}, u32[]{:S(2)}) %copy-start.2) | copy-done | bytes 524312
  5.1 0.0 copy-start.3
  5.1 0.7 copy-done.3
  5.9 0.0 copy-start.4
  5.9 0.7 copy-done.4
  6.5 0.0 copy-start.5
  6.5 0.7 copy-done.5
  7.2 0.0 copy-start.6
  7.2 0.7 copy-done.6
  7.8 89.2 %yee.1 = (f32[1,6,16,64,128]{4,3,2,1,0:T(8,128)S(1)}, f32[1,6,16,64,128]{4,3,2,1,0:T(8,128)S(1)}, f32[8,128]{1,0:T(8,128)S(1)}, f32[8,128]{1,0:T(8,128)S(1)}) custom-call(s32[1,2]{1,0:T(1,128)S(1)} %copy-done.4, f32[3]{0:T(128)S(1)} %copy-done.5, f32[1]{0:T(128)S(6)} %copy.14.absorption_peak, f32[10]{0:T(128)S(1)} %copy-done.6, ...), custom_call_target="tpu_custom_call" | custom-call | tf_op jit(solution)/shard_map/yee/pallas_call | solution.py:632
  97.0 0.7 slice_reduce_fusion
  97.7 1.7 %copy.15 = f32[1,6,16,64,128]{4,3,2,1,0:T(8,128)} copy(f32[1,6,16,64,128]{4,3,2,1,0:T(8,128)S(1)} %get-tuple-element.18) | data formatting | bytes 6291456
  99.3 1.7 %copy.16 = f32[1,6,16,64,128]{4,3,2,1,0:T(8,128)} copy(f32[1,6,16,64,128]{4,3,2,1,0:T(8,128)S(1)} %get-tuple-element.19) | data formatting | bytes 6291456
Async XLA Ops:
  1.3 1.4 %copy-start = (bf16[1,6,16,64,128]{4,3,2,1,0:T(8,128)(2,1)S(1)}, bf16[1,6,16,64,128]{4,3,2,1,0:T(8,128)(2,1)}, u32[]{:S(2)}) copy-start(bf16[1,6,16,64,128]{4,3,2,1,0:T(8,128)(2,1)} %e_in.1) | copy-start | bytes 4718596
  2.7 1.4 %copy-start.1 = (bf16[1,6,16,64,128]{4,3,2,1,0:T(8,128)(2,1)S(1)}, bf16[1,6,16,64,128]{4,3,2,1,0:T(8,128)(2,1)}, u32[]{:S(2)}) copy-start(bf16[1,6,16,64,128]{4,3,2,1,0:T(8,128)(2,1)} %h_in.1) | copy-start | bytes 4718596
  4.1 1.0 %copy-start.2 = (s32[16,64,128]{2,1,0:T(8,128)S(1)}, s32[16,64,128]{2,1,0:T(8,128)}, u32[]{:S(2)}) copy-start(s32[16,64,128]{2,1,0:T(8,128)} %material.1) | copy-start | bytes 1572868
  5.1 0.7 copy-start.3
  5.9 0.7 copy-start.4
  6.5 0.7 copy-start.5
  7.2 0.7 copy-start.6

commit v3 on v2

--- a/solution.py
+++ b/solution.py
@@ -21,10 +21,10 @@
 
 def kernel(
     sizes,
-    bloch,
-    permittivity,
+    bloch_in,
+    permittivity_in,
     absorption_peak,
-    waveform,
+    waveform_in,
     sheet_in,
     material,
     e_in,
@@ -33,6 +33,9 @@
     h_out,
     reflected_out,
     mean_out,
+    bloch,
+    permittivity,
+    waveform,
     ef,
     hf,
     e_low,
@@ -68,6 +71,7 @@
     slab_recv,
     point_send,
     point_recv,
+    hello,
 ):
     points, slabs, rows, width, depth = sizes
     ka = lax.axis_index("ka")
@@ -80,14 +84,39 @@
     inside = pl.ds(TILE, width)
     whole = pl.ds(0, width)
 
+    z_above_1 = lax.rem(ka + 4, points)
+    z_below_1 = lax.rem(ka + points - 4, points)
+    z_above_2 = lax.rem(ka + 8, points)
+    z_below_2 = lax.rem(ka + points - 8, points)
+    core_peer = ka + 1 - 2 * lax.rem(ka, 2)
+    x_peer = ka + 2 - 4 * lax.rem(ka // 2, 2)
+
     barrier = pltpu.get_barrier_semaphore()
-    for other in (up, down):
-        pl.semaphore_signal(barrier, inc=1, device_id=(ka, other), device_id_type=MESH)
-
-    def greet(offset, carry):
-        peer = lax.rem(ka + offset, points)
-        pl.semaphore_signal(barrier, inc=1, device_id=(peer, sp), device_id_type=MESH)
-        return carry
+    near = [(ka, up), (ka, down)]
+    near += [(peer, sp) for peer in (z_above_1, z_below_1, core_peer, x_peer)]
+    for device in near:
+        pl.semaphore_signal(barrier, inc=1, device_id=device, device_id_type=MESH)
+
+    rounds = [
+        ((0, z_above_1), (1, z_below_1)),
+        ((2, z_above_2), (3, z_below_2)),
+        ((4, core_peer),),
+        ((5, x_peer),),
+    ]
+
+    def greet(step):
+        for index in range(len(rounds) + 1):
+
+            @pl.when(step == index)
+            def _():
+                if index > 0:
+                    for place, _peer in rounds[index - 1]:
+                        pl.semaphore_wait(hello.at[place], 1)
+                if index < len(rounds):
+                    for place, peer in rounds[index]:
+                        pl.semaphore_signal(
+                            hello.at[place], inc=1, device_id=(peer, sp), device_id_type=MESH
+                        )
 
     def load(source, target, index):
         copy = pltpu.make_async_copy(source, target, load_sem.at[index])
@@ -103,7 +132,11 @@
     load_e = load(e_in.at[0, :, middle], e_low.at[:, middle], 5)
     load_h = load(h_in.at[0, :, pl.ds(0, last)], h_low.at[:, pl.ds(0, last)], 6)
     load_mat = load(material.at[pl.ds(0, last)], mat.at[pl.ds(0, last)], 7)
-    lax.fori_loop(1, points, greet, 0)
+    small = [
+        load(bloch_in, bloch, 8),
+        load(permittivity_in, permittivity, 9),
+        load(waveform_in, waveform, 10),
+    ]
 
     def remote(source, target, send, recv, other):
         return pltpu.make_async_remote_copy(
@@ -175,7 +208,7 @@
     load_mat_last.wait()
     my_kind[...] = mat[last].astype(F32)
     load_sheet.wait()
-    pl.semaphore_wait(barrier, points + 1)
+    pl.semaphore_wait(barrier, len(near))
     extras[0].start()
     for chunk in range(tiles):
         copy_up(0, chunk).start()
@@ -183,6 +216,8 @@
         copy_ghost(chunk).start()
     extras[1].start()
     extras[2].start()
+    for copy in small:
+        copy.wait()
 
     angle_x = jnp.full((1, depth), 2.0 * jnp.pi * bloch[0, 0].astype(F32) / MPHASE, F32)
     angle_y = jnp.full((1, depth), 2.0 * jnp.pi * bloch[0, 1].astype(F32) / MPHASE, F32)
@@ -490,6 +525,7 @@
                 add_power(0, x)
 
         begin_magnetic()
+        greet(step)
         for chunk in range(tiles):
 
             @pl.when(step == 0)
@@ -549,11 +585,12 @@
     add_power(NSNAP - 1, 0)
     add_power(NSNAP - 1, last)
 
-    row_index = lax.broadcasted_iota(jnp.int32, (TILE, depth), 0)
     at_monitor = lane == PML + 6
-    mine = jnp.zeros((TILE, depth), F32)
+    lane_row = lax.broadcasted_iota(jnp.int32, (1, depth), 1)
+    mine = jnp.zeros((1, depth), F32)
     for snap in range(NSNAP):
-        mine = jnp.where(row_index == snap, jnp.sum(jnp.where(at_monitor, totals[snap], 0.0)), mine)
+        power = jnp.sum(jnp.where(at_monitor, totals[snap], 0.0))
+        mine = jnp.where(lane_row == snap, power, mine)
     slab_sums[0] = mine
 
     def slab_copy(offset):
@@ -610,6 +647,10 @@
     mean_out[...] = total / points
 
 
+def in_hbm(values):
+    return pltpu.with_memory_space_constraint(values, pltpu.HBM)
+
+
 def on_device(
     bloch_index,
     material,
@@ -624,22 +665,24 @@
     slabs = lax.axis_size("sp")
     points = lax.axis_size("ka")
     tiles = width // TILE
-    smem = pl.BlockSpec(memory_space=pltpu.SMEM)
     vmem = pl.BlockSpec(memory_space=pltpu.VMEM)
     hbm = pl.BlockSpec(memory_space=pltpu.HBM)
     dma = pltpu.SemaphoreType.DMA
-    tile = jax.ShapeDtypeStruct((TILE, depth), F32)
+    row = jax.ShapeDtypeStruct((1, depth), F32)
     electric_out, magnetic_out, reflected, mean = pl.pallas_call(
         functools.partial(kernel, (points, slabs, rows, width, depth)),
         out_shape=(
             jax.ShapeDtypeStruct(electric_in.shape, F32),
             jax.ShapeDtypeStruct(magnetic_in.shape, F32),
-            tile,
-            tile,
+            row,
+            row,
         ),
-        in_specs=[smem, smem, smem, smem, hbm, hbm, hbm, hbm],
+        in_specs=[hbm, hbm, pl.BlockSpec(memory_space=pltpu.SMEM)] + [hbm] * 5,
         out_specs=(vmem, vmem, vmem, vmem),
         scratch_shapes=[
+            pltpu.SMEM(bloch_index.shape, jnp.int32),
+            pltpu.SMEM(permittivity.shape, F32),
+            pltpu.SMEM(waveform.shape, F32),
             pltpu.VMEM((6, rows, width + TILE, depth), F32),
             pltpu.VMEM((6, rows, width + TILE, depth), F32),
             pltpu.VMEM((6, rows, width, depth), jnp.bfloat16),
@@ -660,9 +703,9 @@
             pltpu.VMEM((2, width, depth), F32),
             pltpu.VMEM((width, depth), F32),
             pltpu.VMEM((NSNAP, TILE, depth), F32),
-            pltpu.VMEM((slabs, TILE, depth), F32),
-            pltpu.VMEM((points, TILE, depth), F32),
-            dma((8,)),
+            pltpu.VMEM((slabs, 1, depth), F32),
+            pltpu.VMEM((points, 1, depth), F32),
+            dma((11,)),
             dma((tiles,)),
             dma((2, tiles)),
             dma((tiles,)),
@@ -675,22 +718,23 @@
             dma((slabs,)),
             dma((points,)),
             dma((points,)),
+            pltpu.SemaphoreType.REGULAR((6,)),
         ],
         compiler_params=pltpu.CompilerParams(
             collective_id=0, has_side_effects=True, vmem_limit_bytes=32 * 2**20
         ),
         name="yee",
     )(
-        bloch_index,
-        permittivity,
+        in_hbm(bloch_index),
+        in_hbm(permittivity),
         absorption_peak,
-        waveform,
-        source_sheet,
-        material,
-        electric_in,
-        magnetic_in,
+        in_hbm(waveform),
+        in_hbm(source_sheet),
+        in_hbm(material),
+        in_hbm(electric_in),
+        in_hbm(magnetic_in),
     )
-    return (electric_out, magnetic_out, reflected[None, :NSNAP, 0], mean[:NSNAP, 0])
+    return (electric_out, magnetic_out, reflected[:, :NSNAP], mean[0, :NSNAP])
 
 
 def solution(mesh):

time: 101 us -> 93.6 us (0.927)
  local copies, waits for them, and re-layouts: 10.5 us -> 4.35 us
  Pallas kernels: 89.2 us -> 87.8 us
    unnamed x16 -> x3, local copies, waits for them, and re-layouts: 9.86 us -> 3.84 us
    pallas_call x1, Pallas kernels: 89.2 us -> 87.8 us  [on_device(): pl.pallas_call(functools.partial(kernel, (points, slabs, rows, width, dep...]
where the time goes in v3:
time: 93.6 us; the launch traced here: 93.5 us
  Pallas kernels  87.8 us (94%)
  local copies, waits for them, and re-layouts  4.35 us (5%)
  between operations  1.29 us (1%)
    pallas_call x1, Pallas kernels, on_device(): pl.pallas_call(functools.partial(kernel, (points, slabs, rows, width, dep...  87.8 us
    unnamed x3, local copies, waits for them, and re-layouts  3.84 us

profile of v3, /device:TPU:1, one launch (start us, length us, event | category | flops | bytes accessed | tf_op | source)
XLA Modules:
  0.0 93.5 jit_solution(15176894158297371092)
XLA Ops:
  1.3 87.8 %yee.1 = (f32[1,6,16,64,128]{4,3,2,1,0:T(8,128)S(1)}, f32[1,6,16,64,128]{4,3,2,1,0:T(8,128)S(1)}, f32[1,128]{1,0:T(1,128)S(1)}, f32[1,128]{1,0:T(1,128)S(1)}) custom-call(s32[1,2]{1,0:T(1,128)} %bloch_in.1, f32[3]{0:T(128)} %permittivity_in.1, f32[1]{0:T(128)S(6)} %copy.15.absorption_peak, f32[10]{0:T(128)} %waveform_in.1, f32[1,2,16,64]{3,2,1,0:T(8,128)} %sheet_in.1, ...), custom_call_target="tpu_custom_call" | custom-call | tf_op jit(solution)/shard_map/yee/pallas_call | solution.py:672
  89.1 0.5 slice_bitcast_fusion
  89.6 1.7 %copy.16 = f32[1,6,16,64,128]{4,3,2,1,0:T(8,128)} copy(f32[1,6,16,64,128]{4,3,2,1,0:T(8,128)S(1)} %get-tuple-element.16) | data formatting | bytes 6291456
  91.3 1.7 %copy.17 = f32[1,6,16,64,128]{4,3,2,1,0:T(8,128)} copy(f32[1,6,16,64,128]{4,3,2,1,0:T(8,128)S(1)} %get-tuple-element.17) | data formatting | bytes 6291456
  93.0 0.5 copy.18

commit v4 on v3

--- a/solution.py
+++ b/solution.py
@@ -31,8 +31,7 @@
     h_in,
     e_out,
     h_out,
-    reflected_out,
-    mean_out,
+    sums_out,
     bloch,
     permittivity,
     waveform,
@@ -56,8 +55,8 @@
     ghost_sheet,
     my_kind,
     totals,
-    slab_sums,
-    point_sums,
+    plane_sums,
+    height_sums,
     load_sem,
     up_send,
     up_recv,
@@ -67,10 +66,10 @@
     ghost_recv,
     extra_send,
     extra_recv,
-    slab_send,
-    slab_recv,
-    point_send,
-    point_recv,
+    plane_send,
+    plane_recv,
+    height_send,
+    height_recv,
     hello,
 ):
     points, slabs, rows, width, depth = sizes
@@ -81,6 +80,8 @@
     tiles = width // TILE
     last = rows - 1
     steps = NSNAP * INTERVAL
+    heights = points // 4
+    plane = 4 * slabs
     inside = pl.ds(TILE, width)
     whole = pl.ds(0, width)
 
@@ -97,26 +98,28 @@
     for device in near:
         pl.semaphore_signal(barrier, inc=1, device_id=device, device_id_type=MESH)
 
-    rounds = [
-        ((0, z_above_1), (1, z_below_1)),
-        ((2, z_above_2), (3, z_below_2)),
-        ((4, core_peer),),
-        ((5, x_peer),),
-    ]
+    greetings = {
+        0: ((), ((0, z_above_1), (1, z_below_1))),
+        1: ((0, 1), ((2, z_above_2), (3, z_below_2))),
+        2: ((2, 3), ()),
+        5: ((), ((4, core_peer),)),
+        6: ((4,), ((5, x_peer),)),
+        7: ((5,), ()),
+    }
+
+    def exchange_greetings(index):
+        waits, signals = greetings[index]
+        for place in waits:
+            pl.semaphore_wait(hello.at[place], 1)
+        for place, peer in signals:
+            pl.semaphore_signal(
+                hello.at[place], inc=1, device_id=(peer, sp), device_id_type=MESH
+            )
 
     def greet(step):
-        for index in range(len(rounds) + 1):
-
-            @pl.when(step == index)
-            def _():
-                if index > 0:
-                    for place, _peer in rounds[index - 1]:
-                        pl.semaphore_wait(hello.at[place], 1)
-                if index < len(rounds):
-                    for place, peer in rounds[index]:
-                        pl.semaphore_signal(
-                            hello.at[place], inc=1, device_id=(peer, sp), device_id_type=MESH
-                        )
+        for index in greetings:
+            if index > 0:
+                pl.when(step == index)(functools.partial(exchange_greetings, index))
 
     def load(source, target, index):
         copy = pltpu.make_async_copy(source, target, load_sem.at[index])
@@ -197,25 +200,25 @@
     ]
 
     load_first.wait()
+    for part in range(2, 6):
+        ef[part, 0, whole, :] = e_low[part, 0].astype(F32)
+    pl.semaphore_wait(barrier, len(near))
+    for chunk in range(tiles):
+        copy_down(0, chunk).start()
     load_last.wait()
     for part in range(6):
         ef[part, last, whole, :] = e_low[part, last].astype(F32)
-    for part in range(6):
-        ef[part, 0, whole, :] = e_low[part, 0].astype(F32)
+    extras[0].start()
+    load_mat_last.wait()
+    my_kind[...] = mat[last].astype(F32)
+    extras[1].start()
+    load_sheet.wait()
+    extras[2].start()
     load_h_last.wait()
     for part in range(6):
         hf[part, last, inside, :] = h_low[part, last].astype(F32)
-    load_mat_last.wait()
-    my_kind[...] = mat[last].astype(F32)
-    load_sheet.wait()
-    pl.semaphore_wait(barrier, len(near))
-    extras[0].start()
-    for chunk in range(tiles):
-        copy_up(0, chunk).start()
-        copy_down(0, chunk).start()
-        copy_ghost(chunk).start()
-    extras[1].start()
-    extras[2].start()
+    for part in range(2):
+        ef[part, 0, whole, :] = e_low[part, 0].astype(F32)
     for copy in small:
         copy.wait()
 
@@ -487,15 +490,12 @@
 
     totals[...] = jnp.zeros(totals.shape, F32)
 
-    extras[0].wait()
-    real, imag = rotate((ghost_ex[0, whole, :], ghost_ex[1, whole, :]), start_cos, start_sin)
-    ghost_ex[0, whole, :] = real
-    ghost_ex[1, whole, :] = imag
-    fill_ghost_ex_edge()
-
     def finish_ghost():
-        extras[1].wait()
-        extras[2].wait()
+        for extra in extras:
+            extra.wait()
+        real, imag = rotate((ghost_ex[0, whole, :], ghost_ex[1, whole, :]), start_cos, start_sin)
+        ghost_ex[0, whole, :] = real
+        ghost_ex[1, whole, :] = imag
         for tile in range(tiles):
             where = pl.ds(tile * TILE, TILE)
             kind = ghost_kind[where, :]
@@ -511,13 +511,45 @@
 
     half = tiles // 2
 
+    def between(first, end, part, pieces, row):
+        begin, end = share(first, end, part, pieces)
+        lax.fori_loop(begin, end, row, 0)
+
+    begin_magnetic()
+    exchange_greetings(0)
+    for chunk in range(tiles):
+        copy_down(0, chunk).wait()
+        begin = chunk * TILE
+        where = pl.ds(begin, TILE)
+        beyond = pl.ds(begin + TILE, TILE)
+        ey_up = rotate(pair_of(from_up.at[0], 0, where), end_cos, end_sin)
+        ez_up = rotate(pair_of(from_up.at[0], 2, where), end_cos, end_sin)
+        for part in range(2):
+            h_yz(part, last, begin, ey_up[part], ez_up[part])
+        copy_ghost(chunk).start()
+        for part in range(2):
+            e_yz(
+                part, last, begin, hf[2 + part, last - 1, beyond, :], hf[4 + part, last - 1, beyond, :]
+            )
+        copy_up(1, chunk).start()
+        between(1, last - 1, chunk, tiles, h_row)
+    for chunk in range(tiles):
+        copy_ghost(chunk).wait()
+        begin = chunk * TILE
+        beyond = pl.ds(begin + TILE, TILE)
+        for part in (0, 2):
+            real, imag = rotate(pair_of(ghost_h, part, beyond), start_cos, start_sin)
+            ghost_h[part, beyond, :] = real
+            ghost_h[part + 1, beyond, :] = imag
+        for part in range(2):
+            e_yz(part, 0, begin, ghost_h[part, beyond, :], ghost_h[2 + part, beyond, :])
+        copy_down(1, chunk).start()
+    finish_ghost()
+
     def advance(step, carry):
         slot = lax.rem(step, 2)
-        drive = waveform[jnp.maximum(step - 1, 0)]
-
-        @pl.when(step > 0)
-        def _():
-            finish_electric(drive)
+        drive = waveform[step - 1]
+        finish_electric(drive)
 
         @pl.when(step == INTERVAL)
         def _():
@@ -527,29 +559,13 @@
         begin_magnetic()
         greet(step)
         for chunk in range(tiles):
-
-            @pl.when(step == 0)
-            def _():
-                copy_ghost(chunk).wait()
-                where = pl.ds((chunk + 1) * TILE, TILE)
-                for part in (0, 2):
-                    real, imag = rotate(pair_of(ghost_h, part, where), start_cos, start_sin)
-                    ghost_h[part, where, :] = real
-                    ghost_h[part + 1, where, :] = imag
-
             receive(slot, chunk)
             copy_up(1 - slot, chunk).start()
             copy_down(1 - slot, chunk).start()
             if chunk < half:
-
-                @pl.when(step > 0)
-                def _():
-                    begin, end = share(2, last - 1, chunk, half)
-                    lax.fori_loop(begin, end, functools.partial(e_row, drive), 0)
-
+                between(2, last - 1, chunk, half, functools.partial(e_row, drive))
             else:
-                begin, end = share(1, last - 1, chunk - half, tiles - half)
-                lax.fori_loop(begin, end, h_row, 0)
+                between(1, last - 1, chunk - half, tiles - half, h_row)
 
         @pl.when(step == INTERVAL)
         def _():
@@ -559,13 +575,9 @@
 
             lax.fori_loop(2, last - 1, add, 0)
 
-        @pl.when(step == 0)
-        def _():
-            finish_ghost()
-
         return carry
 
-    lax.fori_loop(0, steps - 1, advance, 0)
+    lax.fori_loop(1, steps - 1, advance, 0)
 
     slot = (steps - 1) % 2
     drive = waveform[steps - 2]
@@ -585,66 +597,76 @@
     add_power(NSNAP - 1, 0)
     add_power(NSNAP - 1, last)
 
-    at_monitor = lane == PML + 6
-    lane_row = lax.broadcasted_iota(jnp.int32, (1, depth), 1)
+    at_row = lax.broadcasted_iota(jnp.int32, (1, depth), 1)
     mine = jnp.zeros((1, depth), F32)
     for snap in range(NSNAP):
-        power = jnp.sum(jnp.where(at_monitor, totals[snap], 0.0))
-        mine = jnp.where(lane_row == snap, power, mine)
-    slab_sums[0] = mine
-
-    def slab_copy(offset):
-        return remote(
-            slab_sums.at[0],
-            slab_sums.at[offset],
-            slab_send.at[offset],
-            slab_recv.at[offset],
-            lax.rem(sp + offset, slabs),
-        )
-
-    def point_copy(offset):
+        power = jnp.sum(totals[snap], axis=0, keepdims=True)
+        moved = pltpu.roll(power, depth - (PML + 6) + snap, 1)
+        mine = jnp.where(at_row == snap, moved, mine)
+    plane_sums[0] = mine
+
+    group = points // heights
+    place = lax.rem(ka, group)
+
+    def plane_copy(index):
+        offset = lax.rem(index + plane // 2, plane - 1) + 1
+        peer = ka - place + lax.rem(place + offset // slabs, group)
         return pltpu.make_async_remote_copy(
-            src_ref=point_sums.at[0],
-            dst_ref=point_sums.at[offset],
-            send_sem=point_send.at[offset],
-            recv_sem=point_recv.at[offset],
-            device_id=(lax.rem(ka + offset, points), sp),
+            src_ref=plane_sums.at[0],
+            dst_ref=plane_sums.at[offset],
+            send_sem=plane_send.at[offset],
+            recv_sem=plane_recv.at[offset],
+            device_id=(peer, lax.rem(sp + lax.rem(offset, slabs), slabs)),
             device_id_type=MESH,
         )
 
+    def height_copy(index):
+        offset = lax.rem(index + heights // 2 - 1, heights - 1) + 1
+        return pltpu.make_async_remote_copy(
+            src_ref=height_sums.at[0],
+            dst_ref=height_sums.at[offset],
+            send_sem=height_send.at[offset],
+            recv_sem=height_recv.at[offset],
+            device_id=(lax.rem(ka + group * offset, points), sp),
+            device_id_type=MESH,
+        )
+
     def started(copy):
-        def start(offset, carry):
-            copy(offset).start()
+        def start(index, carry):
+            copy(index).start()
             return carry
 
         return start
 
     def waited(copy):
-        def wait(offset, carry):
-            copy(offset).wait()
+        def wait(index, carry):
+            copy(index).wait()
             return carry
 
         return wait
 
-    lax.fori_loop(1, slabs, started(slab_copy), 0)
+    lax.fori_loop(0, plane - 1, started(plane_copy), 0)
     for x in (0, last):
         for part in range(6):
             e_out[0, part, x] = ef[part, x, whole, :]
     for part in range(6):
         h_out[0, part, last] = hf[part, last, inside, :]
-    lax.fori_loop(1, slabs, waited(slab_copy), 0)
-    total = slab_sums[0]
+    lax.fori_loop(0, plane - 1, waited(plane_copy), 0)
+    slab_total = plane_sums[0]
     for offset in range(1, slabs):
-        total = total + slab_sums[offset]
-    total = total / (rows * slabs * width)
-    point_sums[0] = total
-    reflected_out[...] = total
-    lax.fori_loop(1, points, started(point_copy), 0)
-    lax.fori_loop(1, points, waited(point_copy), 0)
-    total = point_sums[0]
-    for offset in range(1, points):
-        total = total + point_sums[offset]
-    mean_out[...] = total / points
+        slab_total = slab_total + plane_sums[offset]
+    total = slab_total
+    for offset in range(slabs, plane):
+        total = total + plane_sums[offset]
+    height_sums[0] = total
+    lax.fori_loop(0, heights - 1, started(height_copy), 0)
+    cells = rows * slabs * width
+    sums_out[pl.ds(0, 1), :] = slab_total / cells
+    lax.fori_loop(0, heights - 1, waited(height_copy), 0)
+    total = height_sums[0]
+    for offset in range(1, heights):
+        total = total + height_sums[offset]
+    sums_out[pl.ds(1, 1), :] = total / cells / points
 
 
 def in_hbm(values):
@@ -668,17 +690,15 @@
     vmem = pl.BlockSpec(memory_space=pltpu.VMEM)
     hbm = pl.BlockSpec(memory_space=pltpu.HBM)
     dma = pltpu.SemaphoreType.DMA
-    row = jax.ShapeDtypeStruct((1, depth), F32)
-    electric_out, magnetic_out, reflected, mean = pl.pallas_call(
+    electric_out, magnetic_out, sums = pl.pallas_call(
         functools.partial(kernel, (points, slabs, rows, width, depth)),
         out_shape=(
             jax.ShapeDtypeStruct(electric_in.shape, F32),
             jax.ShapeDtypeStruct(magnetic_in.shape, F32),
-            row,
-            row,
+            jax.ShapeDtypeStruct((2, depth), F32),
         ),
         in_specs=[hbm, hbm, pl.BlockSpec(memory_space=pltpu.SMEM)] + [hbm] * 5,
-        out_specs=(vmem, vmem, vmem, vmem),
+        out_specs=(vmem, vmem, vmem),
         scratch_shapes=[
             pltpu.SMEM(bloch_index.shape, jnp.int32),
             pltpu.SMEM(permittivity.shape, F32),
@@ -703,8 +723,8 @@
             pltpu.VMEM((2, width, depth), F32),
             pltpu.VMEM((width, depth), F32),
             pltpu.VMEM((NSNAP, TILE, depth), F32),
-            pltpu.VMEM((slabs, 1, depth), F32),
-            pltpu.VMEM((points, 1, depth), F32),
+            pltpu.VMEM((4 * slabs, 1, depth), F32),
+            pltpu.VMEM((points // 4, 1, depth), F32),
             dma((11,)),
             dma((tiles,)),
             dma((2, tiles)),
@@ -714,10 +734,10 @@
             dma((tiles,)),
             dma((3,)),
             dma((3,)),
-            dma((slabs,)),
-            dma((slabs,)),
-            dma((points,)),
-            dma((points,)),
+            dma((4 * slabs,)),
+            dma((4 * slabs,)),
+            dma((points // 4,)),
+            dma((points // 4,)),
             pltpu.SemaphoreType.REGULAR((6,)),
         ],
         compiler_params=pltpu.CompilerParams(
@@ -734,7 +754,7 @@
         in_hbm(electric_in),
         in_hbm(magnetic_in),
     )
-    return (electric_out, magnetic_out, reflected[:, :NSNAP], mean[0, :NSNAP])
+    return (electric_out, magnetic_out, sums[:1, :NSNAP], sums[1, :NSNAP])
 
 
 def solution(mesh):

time: 93.6 us -> 91.1 us (0.973)
  Pallas kernels: 87.8 us -> 85.8 us
    pallas_call x1, Pallas kernels: 87.8 us -> 85.8 us  [on_device(): pl.pallas_call(functools.partial(kernel, (points, slabs, rows, width, dep...]
    unnamed x3 -> x2, local copies, waits for them, and re-layouts: 3.84 us -> 3.33 us
where the time goes in v4:
time: 91.1 us; the launch traced here: 91 us
  Pallas kernels  85.8 us (94%)
  local copies, waits for them, and re-layouts  3.85 us (4%)
  between operations  1.29 us (1%)
    pallas_call x1, Pallas kernels, on_device(): pl.pallas_call(functools.partial(kernel, (points, slabs, rows, width, dep...  85.8 us
    unnamed x2, local copies, waits for them, and re-layouts  3.33 us

profile of v4, /device:TPU:1, one launch (start us, length us, event | category | flops | bytes accessed | tf_op | source)
XLA Modules:
  0.0 91.0 jit_solution(4154569206860448014)
XLA Ops:
  1.3 85.8 %yee.1 = (f32[1,6,16,64,128]{4,3,2,1,0:T(8,128)S(1)}, f32[1,6,16,64,128]{4,3,2,1,0:T(8,128)S(1)}, f32[2,128]{1,0:T(2,128)S(1)}) custom-call(s32[1,2]{1,0:T(1,128)} %bloch_in.1, f32[3]{0:T(128)} %permittivity_in.1, f32[1]{0:T(128)S(6)} %copy.14.absorption_peak, f32[10]{0:T(128)} %waveform_in.1, f32[1,2,16,64]{3,2,1,0:T(8,128)} %sheet_in.1, ...), custom_call_target="tpu_custom_call" | custom-call | tf_op jit(solution)/shard_map/yee/pallas_call | solution.py:693
  87.1 0.5 slice_bitcast_fusion
  87.6 1.7 %copy.15 = f32[1,6,16,64,128]{4,3,2,1,0:T(8,128)} copy(f32[1,6,16,64,128]{4,3,2,1,0:T(8,128)S(1)} %get-tuple-element.16) | data formatting | bytes 6291456
  89.3 1.7 %copy.16 = f32[1,6,16,64,128]{4,3,2,1,0:T(8,128)} copy(f32[1,6,16,64,128]{4,3,2,1,0:T(8,128)S(1)} %get-tuple-element.17) | data formatting | bytes 6291456

commit v5 on v4

--- a/solution.py
+++ b/solution.py
@@ -71,6 +71,7 @@
     height_send,
     height_recv,
     hello,
+    pace,
 ):
     points, slabs, rows, width, depth = sizes
     ka = lax.axis_index("ka")
@@ -435,11 +436,10 @@
         add_power(NSNAP - 1, x)
         return carry
 
-    def e_x_ends(drive):
-        for x in (0, last):
-            for tile in range(tiles):
-                for part in range(2):
-                    e_x(part, x, tile * TILE, drive)
+    def e_x_plane(x, drive):
+        for tile in range(tiles):
+            for part in range(2):
+                e_x(part, x, tile * TILE, drive)
 
     def finish_electric(drive):
         fill_h_edge(last, (4,))
@@ -448,7 +448,8 @@
             for part in range(2):
                 ghost_e_x(part, tile * TILE, drive)
         fill_ghost_ex_edge()
-        e_x_ends(drive)
+        e_x_plane(0, drive)
+        e_x_plane(last, drive)
         fill_e_edge(0)
         fill_e_edge(last)
         e_row(drive, 1, 0)
@@ -559,9 +560,21 @@
         begin_magnetic()
         greet(step)
         for chunk in range(tiles):
+
+            if chunk == 0:
+
+                @pl.when(step > 1)
+                def _():
+                    pl.semaphore_wait(pace, 1)
             receive(slot, chunk)
             copy_up(1 - slot, chunk).start()
             copy_down(1 - slot, chunk).start()
+
+            if chunk == tiles - 1:
+
+                @pl.when(step < steps - 2)
+                def _():
+                    pl.semaphore_signal(pace, inc=1, device_id=(core_peer, sp), device_id_type=MESH)
             if chunk < half:
                 between(2, last - 1, chunk, half, functools.partial(e_row, drive))
             else:
@@ -590,10 +603,11 @@
             h_out[0, part, x] = hf[part, x, inside, :]
     final = waveform[steps - 1]
     lax.fori_loop(1, last, functools.partial(e_row_out, final), 0)
+    e_x_plane(0, final)
     for chunk in range(tiles):
         receive(slot, chunk)
     fill_h_edge(last, (4,))
-    e_x_ends(final)
+    e_x_plane(last, final)
     add_power(NSNAP - 1, 0)
     add_power(NSNAP - 1, last)
 
@@ -614,8 +628,8 @@
         return pltpu.make_async_remote_copy(
             src_ref=plane_sums.at[0],
             dst_ref=plane_sums.at[offset],
-            send_sem=plane_send.at[offset],
-            recv_sem=plane_recv.at[offset],
+            send_sem=plane_send,
+            recv_sem=plane_recv,
             device_id=(peer, lax.rem(sp + lax.rem(offset, slabs), slabs)),
             device_id_type=MESH,
         )
@@ -625,8 +639,8 @@
         return pltpu.make_async_remote_copy(
             src_ref=height_sums.at[0],
             dst_ref=height_sums.at[offset],
-            send_sem=height_send.at[offset],
-            recv_sem=height_recv.at[offset],
+            send_sem=height_send,
+            recv_sem=height_recv,
             device_id=(lax.rem(ka + group * offset, points), sp),
             device_id_type=MESH,
         )
@@ -638,12 +652,9 @@
 
         return start
 
-    def waited(copy):
-        def wait(index, carry):
-            copy(index).wait()
-            return carry
-
-        return wait
+    def wait_all(sums, count, semaphore):
+        others = sums.at[pl.ds(1, count - 1)]
+        pltpu.make_async_copy(others, others, semaphore).wait()
 
     lax.fori_loop(0, plane - 1, started(plane_copy), 0)
     for x in (0, last):
@@ -651,7 +662,7 @@
             e_out[0, part, x] = ef[part, x, whole, :]
     for part in range(6):
         h_out[0, part, last] = hf[part, last, inside, :]
-    lax.fori_loop(0, plane - 1, waited(plane_copy), 0)
+    wait_all(plane_sums, plane, plane_recv)
     slab_total = plane_sums[0]
     for offset in range(1, slabs):
         slab_total = slab_total + plane_sums[offset]
@@ -662,11 +673,13 @@
     lax.fori_loop(0, heights - 1, started(height_copy), 0)
     cells = rows * slabs * width
     sums_out[pl.ds(0, 1), :] = slab_total / cells
-    lax.fori_loop(0, heights - 1, waited(height_copy), 0)
+    wait_all(plane_sums, plane, plane_send)
+    wait_all(height_sums, heights, height_recv)
     total = height_sums[0]
     for offset in range(1, heights):
         total = total + height_sums[offset]
     sums_out[pl.ds(1, 1), :] = total / cells / points
+    wait_all(height_sums, heights, height_send)
 
 
 def in_hbm(values):
@@ -734,11 +747,12 @@
             dma((tiles,)),
             dma((3,)),
             dma((3,)),
-            dma((4 * slabs,)),
-            dma((4 * slabs,)),
-            dma((points // 4,)),
-            dma((points // 4,)),
+            dma,
+            dma,
+            dma,
+            dma,
             pltpu.SemaphoreType.REGULAR((6,)),
+            pltpu.SemaphoreType.REGULAR,
         ],
         compiler_params=pltpu.CompilerParams(
             collective_id=0, has_side_effects=True, vmem_limit_bytes=32 * 2**20

time: 91.1 us -> 88.7 us (0.974)
  Pallas kernels: 85.8 us -> 83.5 us
    pallas_call x1, Pallas kernels: 85.8 us -> 83.5 us  [on_device(): pl.pallas_call(functools.partial(kernel, (points, slabs, rows, width, dep...]
where the time goes in v5:
time: 88.7 us
  Pallas kernels  83.5 us (94%)
  local copies, waits for them, and re-layouts  3.85 us (4%)
  between operations  1.29 us (1%)
    pallas_call x1, Pallas kernels, on_device(): pl.pallas_call(functools.partial(kernel, (points, slabs, rows, width, dep...  83.5 us
    unnamed x2, local copies, waits for them, and re-layouts  3.33 us

profile of v5, /device:TPU:1, one launch (start us, length us, event | category | flops | bytes accessed | tf_op | source)
XLA Modules:
  0.0 88.7 jit_solution(13788712713499320555)
XLA Ops:
  1.3 83.5 %yee.1 = (f32[1,6,16,64,128]{4,3,2,1,0:T(8,128)S(1)}, f32[1,6,16,64,128]{4,3,2,1,0:T(8,128)S(1)}, f32[2,128]{1,0:T(2,128)S(1)}) custom-call(s32[1,2]{1,0:T(1,128)} %bloch_in.1, f32[3]{0:T(128)} %permittivity_in.1, f32[1]{0:T(128)S(6)} %copy.14.absorption_peak, f32[10]{0:T(128)} %waveform_in.1, f32[1,2,16,64]{3,2,1,0:T(8,128)} %sheet_in.1, ...), custom_call_target="tpu_custom_call" | custom-call | tf_op jit(solution)/shard_map/yee/pallas_call | solution.py:706
  84.8 0.5 slice_bitcast_fusion
  85.3 1.7 %copy.15 = f32[1,6,16,64,128]{4,3,2,1,0:T(8,128)} copy(f32[1,6,16,64,128]{4,3,2,1,0:T(8,128)S(1)} %get-tuple-element.16) | data formatting | bytes 6291456
  87.0 1.7 %copy.16 = f32[1,6,16,64,128]{4,3,2,1,0:T(8,128)} copy(f32[1,6,16,64,128]{4,3,2,1,0:T(8,128)S(1)} %get-tuple-element.17) | data formatting | bytes 6291456

commit v6 on v5

--- a/solution.py
+++ b/solution.py
@@ -421,10 +421,10 @@
         fill_e_edge(x)
         return carry
 
-    def add_power(index, x):
+    def add_power(index, x, parts=(0, 1, 2, 3), chosen=range(tiles)):
         total = totals[index]
-        for part in range(4):
-            for tile in range(tiles):
+        for part in parts:
+            for tile in chosen:
                 values = ef[part, x, pl.ds(tile * TILE, TILE), :]
                 total = total + values * values
         totals[index] = total
@@ -604,12 +604,14 @@
     final = waveform[steps - 1]
     lax.fori_loop(1, last, functools.partial(e_row_out, final), 0)
     e_x_plane(0, final)
+    add_power(NSNAP - 1, 0, (0, 1))
     for chunk in range(tiles):
         receive(slot, chunk)
+        for x in (0, last):
+            add_power(NSNAP - 1, x, (2, 3), (chunk,))
     fill_h_edge(last, (4,))
     e_x_plane(last, final)
-    add_power(NSNAP - 1, 0)
-    add_power(NSNAP - 1, last)
+    add_power(NSNAP - 1, last, (0, 1))
 
     at_row = lax.broadcasted_iota(jnp.int32, (1, depth), 1)
     mine = jnp.zeros((1, depth), F32)
@@ -623,19 +625,19 @@
     place = lax.rem(ka, group)
 
     def plane_copy(index):
-        offset = lax.rem(index + plane // 2, plane - 1) + 1
+        offset = (index + plane // 2) % (plane - 1) + 1
         peer = ka - place + lax.rem(place + offset // slabs, group)
         return pltpu.make_async_remote_copy(
             src_ref=plane_sums.at[0],
             dst_ref=plane_sums.at[offset],
             send_sem=plane_send,
             recv_sem=plane_recv,
-            device_id=(peer, lax.rem(sp + lax.rem(offset, slabs), slabs)),
+            device_id=(peer, lax.rem(sp + offset % slabs, slabs)),
             device_id_type=MESH,
         )
 
     def height_copy(index):
-        offset = lax.rem(index + heights // 2 - 1, heights - 1) + 1
+        offset = (index + heights // 2 - 1) % (heights - 1) + 1
         return pltpu.make_async_remote_copy(
             src_ref=height_sums.at[0],
             dst_ref=height_sums.at[offset],
@@ -645,18 +647,12 @@
             device_id_type=MESH,
         )
 
-    def started(copy):
-        def start(index, carry):
-            copy(index).start()
-            return carry
-
-        return start
-
     def wait_all(sums, count, semaphore):
         others = sums.at[pl.ds(1, count - 1)]
         pltpu.make_async_copy(others, others, semaphore).wait()
 
-    lax.fori_loop(0, plane - 1, started(plane_copy), 0)
+    for index in range(plane - 1):
+        plane_copy(index).start()
     for x in (0, last):
         for part in range(6):
             e_out[0, part, x] = ef[part, x, whole, :]
@@ -670,7 +666,8 @@
     for offset in range(slabs, plane):
         total = total + plane_sums[offset]
     height_sums[0] = total
-    lax.fori_loop(0, heights - 1, started(height_copy), 0)
+    for index in range(heights - 1):
+        height_copy(index).start()
     cells = rows * slabs * width
     sums_out[pl.ds(0, 1), :] = slab_total / cells
     wait_all(plane_sums, plane, plane_send)

time: 88.7 us -> 88.2 us (level)
  no operation moved by 1% of the time
where the time goes in v6:
time: 88.2 us; the launch traced here: 88.1 us
  Pallas kernels  83 us (94%)
  local copies, waits for them, and re-layouts  3.85 us (4%)
  between operations  1.29 us (1%)
    pallas_call x1, Pallas kernels, on_device(): pl.pallas_call(functools.partial(kernel, (points, slabs, rows, width, dep...  83 us
    unnamed x2, local copies, waits for them, and re-layouts  3.33 us

profile of v6, /device:TPU:1, one launch (start us, length us, event | category | flops | bytes accessed | tf_op | source)
XLA Modules:
  0.0 88.1 jit_solution(12528134922955647979)
XLA Ops:
  1.3 83.0 %yee.1 = (f32[1,6,16,64,128]{4,3,2,1,0:T(8,128)S(1)}, f32[1,6,16,64,128]{4,3,2,1,0:T(8,128)S(1)}, f32[2,128]{1,0:T(2,128)S(1)}) custom-call(s32[1,2]{1,0:T(1,128)} %bloch_in.1, f32[3]{0:T(128)} %permittivity_in.1, f32[1]{0:T(128)S(6)} %copy.14.absorption_peak, f32[10]{0:T(128)} %waveform_in.1, f32[1,2,16,64]{3,2,1,0:T(8,128)} %sheet_in.1, ...), custom_call_target="tpu_custom_call" | custom-call | tf_op jit(solution)/shard_map/yee/pallas_call | solution.py:703
  84.3 0.5 slice_bitcast_fusion
  84.8 1.7 %copy.15 = f32[1,6,16,64,128]{4,3,2,1,0:T(8,128)} copy(f32[1,6,16,64,128]{4,3,2,1,0:T(8,128)S(1)} %get-tuple-element.16) | data formatting | bytes 6291456
  86.5 1.7 %copy.16 = f32[1,6,16,64,128]{4,3,2,1,0:T(8,128)} copy(f32[1,6,16,64,128]{4,3,2,1,0:T(8,128)S(1)} %get-tuple-element.17) | data formatting | bytes 6291456
